TPU v7x, 256 devices: a 4x2x16 block of a 4x16x16 slice. The times are simulated.
256 devices in a mesh: grp: 2 (over y), seq: 16 (over z), ch: 4 (over x), col: 2 (over core).
Axes of the slice: x: 4, y: 2, z: 16, core: 2. Of those that a mesh axis runs over, the one named last changes fastest.
The devices are a block of a 4x16x16 slice.
Arguments:
- latent: bfloat16 [32, 16, 16, 512], P('grp', 'seq', 'col', 'ch'), parts along dimension 0, may hold values from -8 to 8, as said below
- mid_gain: float32 [512], P('ch'), may hold values from 0.25 to 1.75
- mid_bias: float32 [512], P('ch'), may hold values from -3 to 3
- mid_weight: bfloat16 [3, 3, 3, 512, 512], P(None, None, None, None, 'ch'), may hold values from -0.0546875 to 0.0546875
- mid_conv_bias: float32 [512], P('ch'), may hold values from -2 to 2
- first_gain: float32 [512], P('ch'), may hold values from 0.25 to 1.75
- first_bias: float32 [512], P('ch'), may hold values from -3 to 3
- first_weight: bfloat16 [3, 3, 3, 512, 512], P(None, None, None, None, 'ch'), may hold values from -0.0546875 to 0.0546875
- first_conv_bias: float32 [512], P('ch'), may hold values from -2 to 2
- second_gain: float32 [512], P('ch'), may hold values from 0.25 to 1.75
- second_bias: float32 [512], P('ch'), may hold values from -3 to 3
- second_weight: bfloat16 [3, 3, 3, 512, 512], P(None, None, None, None, 'ch'), may hold values from -0.0546875 to 0.0546875
- second_conv_bias: float32 [512], P('ch'), may hold values from -2 to 2
Outputs:
- decoded: bfloat16 [64, 16, 16, 512], P(('grp', 'seq'), None, 'col', 'ch'), parts along dimension 0
There are 2 independent parts, one for each index of `grp`. A program takes and returns all parts, laid end to end along the dimension named above; an argument that names none is the same for every part. Nothing has to cross between parts.
Inputs may be any that keep to these rules, and one draw needn't show every extreme that they name: `latent`: each row has its own scale and each row and channel its own offset; values are clipped to the range.
All inputs are finite; a program needn't handle non-finite values.
Results may differ from a plain program's by a relative error of at most 0.0095.
Values may be sent and summed in bfloat16 or wider, within the bound.
A program may use at most 64 MiB of HBM per device.

v0:
```python
import jax
import jax.numpy as jnp
from jax import lax
from jax.sharding import PartitionSpec as P

C = 512
GROUPS = 32


def sent_to_all(shard, axis):
    copies = jnp.broadcast_to(shard, (lax.axis_size(axis), *shard.shape))
    return lax.all_to_all(copies, axis, split_axis=0, concat_axis=0, tiled=True)


def of_everyone(shard, axis):
    return sent_to_all(shard, axis).sum(axis=0)


def packed_total(arrays, axis):
    vector, at, gathered = (jnp.concatenate([a.reshape(-1) for a in arrays]), 0, [])
    total = of_everyone(vector, axis)
    for a in arrays:
        gathered.append(total[at : at + a.size].reshape(a.shape))
        at += a.size
    return tuple(gathered)


def extended_2(shard, sides, width):
    for axis, dim in sides:
        size, length = (lax.axis_size(axis), shard.shape[dim])
        up = [(i, (i + 1) % size) for i in range(size - 1)]
        down = [(j, i) for i, j in up]
        last = lax.slice_in_dim(shard, length - width, length, axis=dim)
        first = lax.slice_in_dim(shard, 0, width, axis=dim)
        before = lax.ppermute(last, axis, up)
        after = lax.ppermute(first, axis, down)
        shard = jnp.concatenate([before, shard, after], axis=dim)
    return shard


def in_order(blocks, dim):
    blocks = jnp.moveaxis(blocks, 0, dim)
    lengths = blocks.shape
    return blocks.reshape(*lengths[:dim], lengths[dim] * lengths[dim + 1], *lengths[dim + 2 :])


def collect(shard, axis, dim):
    blocks = sent_to_all(shard, axis)
    return in_order(blocks, dim)


def shifted(value, axis, steps):
    count = lax.axis_size(axis)
    first, last = (max(0, -steps), min(count, count - steps))
    return lax.ppermute(value, axis, [(source, source + steps) for source in range(first, last)])


def group_norm(field, gain, shift_term):
    values = field.astype(jnp.float32)
    group_size = C // GROUPS
    totals = jnp.sum(values, axis=(0, 1, 2)).reshape(-1, group_size).sum(axis=1)
    squares = jnp.sum(values * values, axis=(0, 1, 2)).reshape(-1, group_size).sum(axis=1)
    totals, squares = packed_total((totals, squares), ("seq", "col"))
    samples = (
        values.shape[0]
        * values.shape[1]
        * values.shape[2]
        * group_size
        * lax.axis_size("seq")
        * lax.axis_size("col")
    )
    group_mean = totals / samples
    spread = squares / samples - group_mean * group_mean
    inverse = 1.0 / jnp.sqrt(spread + 0.01)
    scaled = (values - jnp.repeat(group_mean, group_size)) * jnp.repeat(
        inverse, group_size
    ) * gain + shift_term
    return jax.nn.silu(scaled).astype(jnp.bfloat16)


def spatial_halo(activation):
    return extended_2(activation, (("seq", 1), ("col", 2)), 1)


def causal_pad(extended):
    return jnp.pad(extended, ((2, 0), (0, 0), (0, 0), (0, 0)))


def channel_conv(padded, weight):
    frames_out = padded.shape[0] - 2
    rows_out = padded.shape[1] - 2
    cols_out = padded.shape[2] - 2
    running = jnp.zeros((frames_out, rows_out, cols_out, weight.shape[4]), jnp.float32)
    carried = running
    portion = collect(padded, "ch", 3)
    for tap_time in range(3):
        for tap_row in range(3):
            for tap_col in range(3):
                window = portion[
                    tap_time : tap_time + frames_out,
                    tap_row : tap_row + rows_out,
                    tap_col : tap_col + cols_out,
                ]
                carried = carried + jnp.einsum(
                    "thwc,co->thwo",
                    window,
                    weight[tap_time, tap_row, tap_col],
                    preferred_element_type=jnp.float32,
                )
    return carried


def to_frames(field):
    return lax.all_to_all(field, "seq", split_axis=0, concat_axis=1, tiled=True)


def frames_conv(activation, weight):
    history = shifted(activation, "seq", 1)
    extended = jnp.concatenate([history, activation], axis=0)
    extended = jnp.pad(extended, ((0, 0), (1, 1), (0, 0), (0, 0)))
    extended = extended_2(extended, (("col", 2),), 1)
    return channel_conv(extended, weight)


def rows_conv(activation, weight):
    return channel_conv(causal_pad(spatial_halo(activation)), weight)


def body(
    latent,
    mid_gain,
    mid_bias,
    mid_weight,
    mid_conv_bias,
    first_gain,
    first_bias,
    first_weight,
    first_conv_bias,
    second_gain,
    second_bias,
    second_weight,
    second_conv_bias,
):
    mid_act = group_norm(latent, mid_gain, mid_bias)
    mixed = rows_conv(mid_act, mid_weight)
    middle = (latent.astype(jnp.float32) + mixed + mid_conv_bias).astype(jnp.bfloat16)
    owned = to_frames(middle)
    doubled = jnp.repeat(owned, 2, axis=0)
    first_act = group_norm(doubled, first_gain, first_bias)
    hidden = (frames_conv(first_act, first_weight) + first_conv_bias).astype(jnp.bfloat16)
    second_act = group_norm(hidden, second_gain, second_bias)
    return (
        doubled.astype(jnp.float32) + frames_conv(second_act, second_weight) + second_conv_bias
    ).astype(jnp.bfloat16)


def solution(mesh):
    in_specs = (
        P("grp", "seq", "col", "ch"),
        P("ch"),
        P("ch"),
        P(None, None, None, None, "ch"),
        P("ch"),
        P("ch"),
        P("ch"),
        P(None, None, None, None, "ch"),
        P("ch"),
        P("ch"),
        P("ch"),
        P(None, None, None, None, "ch"),
        P("ch"),
    )
    out_specs = P(("grp", "seq"), None, "col", "ch")
    return jax.shard_map(body, mesh=mesh, in_specs=in_specs, out_specs=out_specs, check_vma=False)
```

profile of v0, /device:TPU:33, one launch (start us, length us, event | category | flops | bytes accessed | tf_op | source)
XLA Modules:
  0.0 210.3 jit_solution(6211185844503411250)
XLA Ops:
  0.0 0.8 convert_reduce_fusion
  1.3 36.8 %all_to_all.42 = f32[32,1,16]{2,1,0:T(1,128)S(1)} all-to-all(f32[32,1,16]{2,1,0:T(1,128)S(1)} %broadcast_in_dim.46), channel_id=1, replica_groups=mesh['grp'=2,'seq'=16,'ch'=4,'col'=2] {'seq','col'}, dimensions={0} | all-to-all | bytes 4096 | tf_op jit(solution)/shard_map/all_to_all | solution.py:12
  38.6 0.8 fusion.243
  39.4 1.3 collective-permute-start.1
  40.7 4.0 %collective-permute-start = (bf16[16,1,8,128]{3,2,0,1:T(8,128)(2,1)S(1)}, bf16[16,1,8,128]{3,2,0,1:T(8,128)(2,1)S(1)}, u32[]{:S(2)}, u32[]{:S(2)}) collective-permute-start(bf16[16,1,8,128]{3,2,0,1:T(8,128)(2,1)S(1)} %fusion.243), channel_id=1, source_target_pairs={{0,8},{8,16},{16,24},{24,32},{32,40},{40,48},{48,56},{56,64},{64,7... | collective-permute-start | bytes 98312 | tf_op jit(solution)/shard_map/ppermute | solution.py:35
  44.8 1.0 collective-permute-done
  45.8 1.3 collective-permute-start.2
  47.1 4.0 %collective-permute-start.3 = (bf16[16,3,1,128]{3,2,0,1:T(2,128)(2,1)S(1)}, bf16[16,3,1,128]{3,2,0,1:T(2,128)(2,1)S(1)}, u32[]{:S(2)}, u32[]{:S(2)}) collective-permute-start(bf16[16,3,1,128]{3,2,0,1:T(2,128)(2,1)S(1)} %get-tuple-element.14), channel_id=1, source_target_pairs={{1,0},{3,2},{5,4},{7,6},{9,8},{11,10},{13,12},{15,14},{17,16},{19,... | collective-permute-start | bytes 36872 | tf_op jit(solution)/shard_map/ppermute | solution.py:36
  51.1 0.8 collective-permute-done.3
  52.3 15.2 %all_to_all.43 = bf16[4,18,3,10,128]{4,1,3,2,0:T(8,128)(2,1)S(1)} all-to-all(bf16[4,18,3,10,128]{4,1,3,2,0:T(8,128)(2,1)S(1)} %broadcast_in_dim.49), channel_id=1, replica_groups=mesh['grp'=2,'seq'=16,'ch'=4,'col'=2] {'ch'}, dimensions={0} | all-to-all | bytes 1105920 | tf_op jit(solution)/shard_map/all_to_all | solution.py:12
  68.0 1.2 fusion.71
  69.2 1.1 convolution_add_fusion.77
  70.3 1.1 convolution_add_fusion.76
  71.4 1.1 convolution_add_fusion.75
  72.5 1.1 convolution_add_fusion.74
  73.6 1.1 convolution_add_fusion.73
  74.7 1.1 convolution_add_fusion.72
  75.7 1.1 convolution_add_fusion.71
  76.8 1.1 convolution_add_fusion.70
  81.3 17.3 %all_to_all.44 = bf16[16,1,8,128]{3,2,1,0:T(8,128)(2,1)S(1)} all-to-all(bf16[16,1,8,128]{3,2,1,0:T(8,128)(2,1)S(1)} %fusion.10), channel_id=1, replica_groups=mesh['grp'=2,'seq'=16,'ch'=4,'col'=2] {'seq'}, dimensions={0} | all-to-all | bytes 65536 | tf_op jit(solution)/shard_map/all_to_all | solution.py:114
  99.3 17.8 %all_to_all.45 = f32[32,1,16]{2,1,0:T(1,128)S(1)} all-to-all(f32[32,1,16]{2,1,0:T(1,128)S(1)} %broadcast_in_dim.50), channel_id=1, replica_groups=mesh['grp'=2,'seq'=16,'ch'=4,'col'=2] {'seq','col'}, dimensions={0} | all-to-all | bytes 4096 | tf_op jit(solution)/shard_map/all_to_all | solution.py:12
  117.5 2.2 %collective-permute-start.4 = (bf16[2,16,8,128]{3,2,1,0:T(8,128)(2,1)S(1)}, bf16[2,16,8,128]{3,2,1,0:T(8,128)(2,1)S(1)}, u32[]{:S(2)}, u32[]{:S(2)}) collective-permute-start(bf16[2,16,8,128]{3,2,1,0:T(8,128)(2,1)S(1)} %multiply_convert_fusion.1), channel_id=1, source_target_pairs={{0,8},{8,16},{16,24},{24,32},{32,40},{40,48},{48,56},{56,64},{64,7... | collective-permute-start | bytes 196616 | tf_op jit(solution)/shard_map/ppermute | solution.py:55
  119.7 1.3 collective-permute-done.4
  121.1 1.3 collective-permute-start.5
  122.4 3.8 %collective-permute-start.6 = (bf16[4,18,1,128]{3,2,1,0:T(2,128)(2,1)S(1)}, bf16[4,18,1,128]{3,2,1,0:T(2,128)(2,1)S(1)}, u32[]{:S(2)}, u32[]{:S(2)}) collective-permute-start(bf16[4,18,1,128]{3,2,1,0:T(2,128)(2,1)S(1)} %get-tuple-element.12), channel_id=1, source_target_pairs={{1,0},{3,2},{5,4},{7,6},{9,8},{11,10},{13,12},{15,14},{17,16},{19,... | collective-permute-start | bytes 55304 | tf_op jit(solution)/shard_map/ppermute | solution.py:36
  126.2 0.8 collective-permute-done.6
  127.5 13.6 %all_to_all.46 = bf16[4,4,18,10,128]{4,1,3,2,0:T(4,128)(2,1)S(1)} all-to-all(bf16[4,4,18,10,128]{4,1,3,2,0:T(4,128)(2,1)S(1)} %broadcast_in_dim.53), channel_id=1, replica_groups=mesh['grp'=2,'seq'=16,'ch'=4,'col'=2] {'ch'}, dimensions={0} | all-to-all | bytes 1474560 | tf_op jit(solution)/shard_map/all_to_all | solution.py:12
  141.8 1.3 fusion.66
  143.1 1.1 convolution_add_fusion.51
  144.2 1.1 convolution_add_fusion.50
  145.4 1.1 convolution_add_fusion.49
  146.5 1.1 convolution_add_fusion.48
  147.7 1.1 convolution_add_fusion.47
  154.5 18.2 %all_to_all.47 = f32[32,1,16]{2,1,0:T(1,128)S(1)} all-to-all(f32[32,1,16]{2,1,0:T(1,128)S(1)} %broadcast_in_dim.54), channel_id=1, replica_groups=mesh['grp'=2,'seq'=16,'ch'=4,'col'=2] {'seq','col'}, dimensions={0} | all-to-all | bytes 4096 | tf_op jit(solution)/shard_map/all_to_all | solution.py:12
  173.2 2.2 %collective-permute-start.7 = (bf16[2,16,8,128]{3,2,1,0:T(8,128)(2,1)S(1)}, bf16[2,16,8,128]{3,2,1,0:T(8,128)(2,1)S(1)}, u32[]{:S(2)}, u32[]{:S(2)}) collective-permute-start(bf16[2,16,8,128]{3,2,1,0:T(8,128)(2,1)S(1)} %multiply_convert_fusion), channel_id=1, source_target_pairs={{0,8},{8,16},{16,24},{24,32},{32,40},{40,48},{48,56},{56,64},{64,7... | collective-permute-start | bytes 196616 | tf_op jit(solution)/shard_map/ppermute | solution.py:55
  175.4 1.3 collective-permute-done.7
  176.8 1.3 collective-permute-start.8
  178.1 3.7 %collective-permute-start.9 = (bf16[4,18,1,128]{3,2,1,0:T(2,128)(2,1)S(1)}, bf16[4,18,1,128]{3,2,1,0:T(2,128)(2,1)S(1)}, u32[]{:S(2)}, u32[]{:S(2)}) collective-permute-start(bf16[4,18,1,128]{3,2,1,0:T(2,128)(2,1)S(1)} %get-tuple-element.10), channel_id=1, source_target_pairs={{1,0},{3,2},{5,4},{7,6},{9,8},{11,10},{13,12},{15,14},{17,16},{19,... | collective-permute-start | bytes 55304 | tf_op jit(solution)/shard_map/ppermute | solution.py:36
  181.9 0.8 collective-permute-done.9
  183.2 13.6 %all_to_all.48 = bf16[4,4,18,10,128]{4,1,3,2,0:T(4,128)(2,1)S(1)} all-to-all(bf16[4,4,18,10,128]{4,1,3,2,0:T(4,128)(2,1)S(1)} %broadcast_in_dim.57), channel_id=1, replica_groups=mesh['grp'=2,'seq'=16,'ch'=4,'col'=2] {'ch'}, dimensions={0} | all-to-all | bytes 1474560 | tf_op jit(solution)/shard_map/all_to_all | solution.py:12
  197.1 0.3 reshape.332
  197.5 1.3 fusion.38
  198.8 1.1 convolution_add_fusion.25
  199.9 1.1 convolution_add_fusion.24
  201.1 1.1 convolution_add_fusion.23
  202.2 1.1 convolution_add_fusion.22
  203.3 1.1 convolution_add_fusion.21
  209.4 0.9 fusion.5
  (147 shorter events, 18.8 us)
Async XLA Ops:
  39.4 5.4 %collective-permute-start.1 = (bf16[16,1,8,128]{3,2,0,1:T(8,128)(2,1)S(1)}, bf16[16,1,8,128]{3,2,0,1:T(8,128)(2,1)S(1)}, u32[]{:S(2)}, u32[]{:S(2)}) collective-permute-start(bf16[16,1,8,128]{3,2,0,1:T(8,128)(2,1)S(1)} %fusion.243), channel_id=1, source_target_pairs={{8,0},{16,8},{24,16},{32,24},{40,32},{48,40},{56,48},{64,56},{72,6... | collective-permute-start | bytes 98312 | tf_op jit(solution)/shard_map/ppermute | solution.py:36
  40.7 5.0 %collective-permute-start = (bf16[16,1,8,128]{3,2,0,1:T(8,128)(2,1)S(1)}, bf16[16,1,8,128]{3,2,0,1:T(8,128)(2,1)S(1)}, u32[]{:S(2)}, u32[]{:S(2)}) collective-permute-start(bf16[16,1,8,128]{3,2,0,1:T(8,128)(2,1)S(1)} %fusion.243), channel_id=1, source_target_pairs={{0,8},{8,16},{16,24},{24,32},{32,40},{40,48},{48,56},{56,64},{64,7... | collective-permute-start | bytes 98312 | tf_op jit(solution)/shard_map/ppermute | solution.py:35
  45.8 5.3 %collective-permute-start.2 = (bf16[16,3,1,128]{3,2,0,1:T(2,128)(2,1)S(1)}, bf16[16,3,1,128]{3,2,0,1:T(2,128)(2,1)S(1)}, u32[]{:S(2)}, u32[]{:S(2)}) collective-permute-start(bf16[16,3,1,128]{3,2,0,1:T(2,128)(2,1)S(1)} %get-tuple-element.13), channel_id=1, source_target_pairs={{0,1},{2,3},{4,5},{6,7},{8,9},{10,11},{12,13},{14,15},{16,17},{18,... | collective-permute-start | bytes 36872 | tf_op jit(solution)/shard_map/ppermute | solution.py:35
  47.1 4.8 %collective-permute-start.3 = (bf16[16,3,1,128]{3,2,0,1:T(2,128)(2,1)S(1)}, bf16[16,3,1,128]{3,2,0,1:T(2,128)(2,1)S(1)}, u32[]{:S(2)}, u32[]{:S(2)}) collective-permute-start(bf16[16,3,1,128]{3,2,0,1:T(2,128)(2,1)S(1)} %get-tuple-element.14), channel_id=1, source_target_pairs={{1,0},{3,2},{5,4},{7,6},{9,8},{11,10},{13,12},{15,14},{17,16},{19,... | collective-permute-start | bytes 36872 | tf_op jit(solution)/shard_map/ppermute | solution.py:36
  68.0 10.0 %copy-start = (bf16[3,3,3,512,128]{4,3,2,1,0:T(8,128)(2,1)S(1)}, bf16[3,3,3,512,128]{4,3,2,1,0:T(8,128)(2,1)}, u32[]{:S(2)}) copy-start(bf16[3,3,3,512,128]{4,3,2,1,0:T(8,128)(2,1)} %param.16) | copy-start | bytes 10616836
  77.9 3.2 %copy-start.3 = (bf16[16,1,8,128]{3,2,1,0:T(8,128)(2,1)S(1)}, bf16[16,1,8,128]{3,2,1,0:T(8,128)(2,1)}, u32[]{:S(2)}) copy-start(bf16[16,1,8,128]{3,2,1,0:T(8,128)(2,1)} %param.13) | copy-start | bytes 98308
  77.9 3.2 %copy-start.8 = (f32[128]{0:T(128)S(1)}, f32[128]{0:T(128)}, u32[]{:S(2)}) copy-start(f32[128]{0:T(128)} %param.17) | copy-start | bytes 1540
  78.3 39.2 %copy-start.4 = (f32[128]{0:T(128)S(1)}, f32[128]{0:T(128)}, u32[]{:S(2)}) copy-start(f32[128]{0:T(128)} %param.19) | copy-start | bytes 1540
  78.3 39.2 %copy-start.5 = (f32[128]{0:T(128)S(1)}, f32[128]{0:T(128)}, u32[]{:S(2)}) copy-start(f32[128]{0:T(128)} %param.18) | copy-start | bytes 1540
  117.5 3.5 %collective-permute-start.4 = (bf16[2,16,8,128]{3,2,1,0:T(8,128)(2,1)S(1)}, bf16[2,16,8,128]{3,2,1,0:T(8,128)(2,1)S(1)}, u32[]{:S(2)}, u32[]{:S(2)}) collective-permute-start(bf16[2,16,8,128]{3,2,1,0:T(8,128)(2,1)S(1)} %multiply_convert_fusion.1), channel_id=1, source_target_pairs={{0,8},{8,16},{16,24},{24,32},{32,40},{40,48},{48,56},{56,64},{64,7... | collective-permute-start | bytes 196616 | tf_op jit(solution)/shard_map/ppermute | solution.py:55
  121.1 5.1 %collective-permute-start.5 = (bf16[4,18,1,128]{3,2,1,0:T(2,128)(2,1)S(1)}, bf16[4,18,1,128]{3,2,1,0:T(2,128)(2,1)S(1)}, u32[]{:S(2)}, u32[]{:S(2)}) collective-permute-start(bf16[4,18,1,128]{3,2,1,0:T(2,128)(2,1)S(1)} %get-tuple-element.11), channel_id=1, source_target_pairs={{0,1},{2,3},{4,5},{6,7},{8,9},{10,11},{12,13},{14,15},{16,17},{18,... | collective-permute-start | bytes 55304 | tf_op jit(solution)/shard_map/ppermute | solution.py:35
  122.4 4.6 %collective-permute-start.6 = (bf16[4,18,1,128]{3,2,1,0:T(2,128)(2,1)S(1)}, bf16[4,18,1,128]{3,2,1,0:T(2,128)(2,1)S(1)}, u32[]{:S(2)}, u32[]{:S(2)}) collective-permute-start(bf16[4,18,1,128]{3,2,1,0:T(2,128)(2,1)S(1)} %get-tuple-element.12), channel_id=1, source_target_pairs={{1,0},{3,2},{5,4},{7,6},{9,8},{11,10},{13,12},{15,14},{17,16},{19,... | collective-permute-start | bytes 55304 | tf_op jit(solution)/shard_map/ppermute | solution.py:36
  141.8 7.0 %copy-start.1 = (bf16[3,3,3,512,128]{4,3,2,1,0:T(8,128)(2,1)S(1)}, bf16[3,3,3,512,128]{4,3,2,1,0:T(8,128)(2,1)}, u32[]{:S(2)}) copy-start(bf16[3,3,3,512,128]{4,3,2,1,0:T(8,128)(2,1)} %param.20) | copy-start | bytes 10616836
  151.2 2.5 %copy-start.9 = (f32[128]{0:T(128)S(1)}, f32[128]{0:T(128)}, u32[]{:S(2)}) copy-start(f32[128]{0:T(128)} %param.21) | copy-start | bytes 1540
  151.5 21.6 %copy-start.6 = (f32[128]{0:T(128)S(1)}, f32[128]{0:T(128)}, u32[]{:S(2)}) copy-start(f32[128]{0:T(128)} %param.23) | copy-start | bytes 1540
  151.5 21.6 %copy-start.7 = (f32[128]{0:T(128)S(1)}, f32[128]{0:T(128)}, u32[]{:S(2)}) copy-start(f32[128]{0:T(128)} %param.22) | copy-start | bytes 1540
  173.2 3.5 %collective-permute-start.7 = (bf16[2,16,8,128]{3,2,1,0:T(8,128)(2,1)S(1)}, bf16[2,16,8,128]{3,2,1,0:T(8,128)(2,1)S(1)}, u32[]{:S(2)}, u32[]{:S(2)}) collective-permute-start(bf16[2,16,8,128]{3,2,1,0:T(8,128)(2,1)S(1)} %multiply_convert_fusion), channel_id=1, source_target_pairs={{0,8},{8,16},{16,24},{24,32},{32,40},{40,48},{48,56},{56,64},{64,7... | collective-permute-start | bytes 196616 | tf_op jit(solution)/shard_map/ppermute | solution.py:55
  176.8 5.1 %collective-permute-start.8 = (bf16[4,18,1,128]{3,2,1,0:T(2,128)(2,1)S(1)}, bf16[4,18,1,128]{3,2,1,0:T(2,128)(2,1)S(1)}, u32[]{:S(2)}, u32[]{:S(2)}) collective-permute-start(bf16[4,18,1,128]{3,2,1,0:T(2,128)(2,1)S(1)} %get-tuple-element.9), channel_id=1, source_target_pairs={{0,1},{2,3},{4,5},{6,7},{8,9},{10,11},{12,13},{14,15},{16,17},{18,... | collective-permute-start | bytes 55304 | tf_op jit(solution)/shard_map/ppermute | solution.py:35
  178.1 4.6 %collective-permute-start.9 = (bf16[4,18,1,128]{3,2,1,0:T(2,128)(2,1)S(1)}, bf16[4,18,1,128]{3,2,1,0:T(2,128)(2,1)S(1)}, u32[]{:S(2)}, u32[]{:S(2)}) collective-permute-start(bf16[4,18,1,128]{3,2,1,0:T(2,128)(2,1)S(1)} %get-tuple-element.10), channel_id=1, source_target_pairs={{1,0},{3,2},{5,4},{7,6},{9,8},{11,10},{13,12},{15,14},{17,16},{19,... | collective-permute-start | bytes 55304 | tf_op jit(solution)/shard_map/ppermute | solution.py:36
  197.5 7.0 %copy-start.2 = (bf16[3,3,3,512,128]{4,3,2,1,0:T(8,128)(2,1)S(1)}, bf16[3,3,3,512,128]{4,3,2,1,0:T(8,128)(2,1)}, u32[]{:S(2)}) copy-start(bf16[3,3,3,512,128]{4,3,2,1,0:T(8,128)(2,1)} %param.24) | copy-start | bytes 10616836
  206.9 2.4 %copy-start.10 = (f32[128]{0:T(128)S(1)}, f32[128]{0:T(128)}, u32[]{:S(2)}) copy-start(f32[128]{0:T(128)} %param.25) | copy-start | bytes 1540
where the time goes:
time: 211 us; the launch traced here: 210 us
  blocking collectives  133 us (63%)
  matrix products  37.8 us (18%)
  starting transfers between devices  25.1 us (12%)
  waiting for transfers between devices  6.12 us (3%)
  local copies, waits for them, and re-layouts  4.03 us (2%)
  other arithmetic  3.7 us (2%)
    all_to_all x6, blocking collectives, sent_to_all(): return lax.all_to_all(copies, axis, split_axis=0, concat_axis=0, tiled=True)  115 us
    dot_general x81, matrix products, channel_conv(): jnp.einsum('thwc,co->thwo', window, weight[tap_time, tap_row, tap_col], p...  37.8 us
    all_to_all x1, blocking collectives, to_frames(): return lax.all_to_all(field, 'seq', split_axis=0, concat_axis=1, tiled=True)  17.3 us
    ppermute x4, starting transfers between devices, extended_2(): after = lax.ppermute(first, axis, down)  12.8 us
    ppermute x4, starting transfers between devices, extended_2(): before = lax.ppermute(last, axis, up)  7.96 us
    ppermute x2, starting transfers between devices, shifted(): lax.ppermute(value, axis, [(source, source + steps) for source in range(f...  4.35 us
  transfers between devices with their start and end apart: 10, of which 6 were waited for; matrix products, arithmetic and copies ran while one was open for 0% of the time, Pallas kernels for 0%

commit v1 on v0

v1 whole, which is shorter than its diff:
```python
import functools

import jax
import jax.numpy as jnp
from jax import lax
from jax.experimental import pallas as pl
from jax.experimental.pallas import tpu as pltpu
from jax.sharding import PartitionSpec as P

MESH = pl.DeviceIdType.MESH
GROUP = 16
LANES = 128
EPS = 0.01
BF = jnp.bfloat16
F32 = jnp.float32


def lane_ids():
    return lax.broadcasted_iota(jnp.int32, (8, LANES), 1)


def row_ids():
    return lax.broadcasted_iota(jnp.int32, (8, LANES), 0)


def group_total(v):
    lane = lane_ids()
    step = GROUP // 2
    while step:
        from_below = pltpu.roll(v, step, 1)
        from_above = pltpu.roll(v, LANES - step, 1)
        v = v + jnp.where((lane & step) != 0, from_below, from_above)
        step //= 2
    return v


def packed_sums(values, x):
    total = jnp.sum(values, axis=0, keepdims=True)
    square = jnp.sum(values * values, axis=0, keepdims=True)
    total = group_total(jnp.broadcast_to(total, (8, LANES)))
    square = group_total(jnp.broadcast_to(square, (8, LANES)))
    slot = lane_ids() & 7
    row = jnp.where(slot == 2 * x, total, jnp.where(slot == 2 * x + 1, square, 0.0))
    return row[0:1]


def affine(row, samples, params, which, nx):
    spread_rows = jnp.broadcast_to(row, (8, LANES))
    picked = jnp.where((lane_ids() & (GROUP - 1)) == row_ids(), spread_rows, 0.0)
    sums = group_total(picked) * (1.0 / samples)
    out = []
    for block in range(nx):
        mean = sums[2 * block : 2 * block + 1]
        square = sums[2 * block + 1 : 2 * block + 2]
        inverse = 1.0 / jnp.sqrt(square - mean * mean + EPS)
        gain = params[block, 2 * which : 2 * which + 1]
        bias = params[block, 2 * which + 1 : 2 * which + 2]
        scale = inverse * gain
        out.append((scale, bias - mean * scale))
    return out


def activate(values, scale, shift):
    u = values * scale.reshape((1,) * (values.ndim - 1) + (LANES,)) + shift.reshape(
        (1,) * (values.ndim - 1) + (LANES,)
    )
    half = 0.5 * u
    return (half + half * jnp.tanh(half)).astype(BF)


def column_sum(y):
    n, cols = y.shape[0], y.shape[1]
    left, mid, right = (y[:, :, i * LANES : (i + 1) * LANES] for i in range(3))
    col = lax.broadcasted_iota(jnp.int32, (n, cols, LANES), 1)
    left = jnp.where(col == 0, 0.0, pltpu.roll(left, 1, 1))
    right = jnp.where(col == cols - 1, 0.0, pltpu.roll(right, cols - 1, 1))
    return left + mid + right


def taps(weight, dt, di):
    base = dt * 9 + di * 3
    return jnp.concatenate([weight[base + dj] for dj in range(3)], axis=1)


def dot(a, b):
    return jnp.dot(a, b, preferred_element_type=F32)


def flat(v):
    return v.reshape(-1, v.shape[-1])


def kernel(
    nz,
    nx,
    lat,
    g0,
    b0,
    w0_hbm,
    c0,
    g1,
    b1,
    w1_hbm,
    c1,
    g2,
    b2,
    w2_hbm,
    c2,
    out,
    w0,
    w1,
    w2,
    params,
    r0,
    x1,
    x2,
    act0,
    act1,
    act2,
    middle,
    hidden,
    give,
    take,
    plane_src,
    plane_in,
    line_src,
    line_in,
    w_sem,
    par_s,
    par_r,
    plane_s,
    plane_r,
    line_s,
    line_r,
    x0_s,
    x0_r,
    z0_s,
    z0_r,
    a_s,
    a_r,
    x1_s,
    x1_r,
    x2_s,
    x2_r,
    e2_s,
    e2_r,
    o_s,
    o_r,
):
    z = lax.axis_index("seq")
    x = lax.axis_index("ch")
    c = lax.axis_index("col")
    half = nz // 2
    samples = float(nz * nz * 16 * GROUP)

    def peer(dz, dx, col):
        return {"seq": lax.rem(z + dz + nz, nz), "ch": lax.rem(x + dx, nx), "col": col}

    def remote(src, dst, s_sem, r_sem, to):
        return pltpu.make_async_remote_copy(
            src_ref=src,
            dst_ref=dst,
            send_sem=s_sem,
            recv_sem=r_sem,
            device_id=to,
            device_id_type=MESH,
        )

    def landed(ref, sem):
        pltpu.make_async_copy(ref, ref, sem).wait()

    loads = [
        pltpu.make_async_copy(a, b, w_sem.at[i])
        for i, (a, b) in enumerate(((w0_hbm, w0), (w1_hbm, w1), (w2_hbm, w2)))
    ]
    for load in loads:
        load.start()

    barrier = pltpu.get_barrier_semaphore()
    greeted = []
    for dz in range(nz):
        greeted.append((dz, 0, 1 - c))
        if dz:
            greeted.append((dz, 0, c))
    for dz in (0, 1, nz - 1):
        for dx in range(1, nx):
            greeted.append((dz, dx, c))
            greeted.append((dz, dx, 1 - c))
    greeted.sort(key=lambda g: -min(g[0], nz - g[0]))
    for dz, dx, col in greeted:
        pl.semaphore_signal(barrier, inc=1, device_id=peer(dz, dx, col), device_id_type=MESH)

    mine = pl.multiple_of(x * 8, 8)
    for i, ref in enumerate((g0, b0, g1, b1, g2, b2)):
        params[x, i : i + 1, :] = ref[...]
    own = lat[...].astype(F32)
    plane_src[0] = packed_sums(flat(own), x)
    own_at = ((nx + x) * 2 + c) * 6
    r0[pl.ds(own_at + 1 - c, 5)] = lat[pl.ds(3 * c, 5)]

    pl.semaphore_wait(barrier, len(greeted))

    def plane_start(stage):
        place = 8 * stage + 2 * x + c
        plane_in[place] = plane_src[stage]
        for dx in range(nx):
            for other in (0, 1):
                if dx == 0 and other == 0:
                    continue
                remote(
                    plane_src.at[stage],
                    plane_in.at[place],
                    plane_s.at[stage],
                    plane_r.at[stage],
                    peer(0, dx, c if other == 0 else 1 - c),
                ).start()

    def line_start(stage):
        landed(plane_in.at[pl.ds(8 * stage, 2 * nx - 1)], plane_r.at[stage])
        row = jnp.sum(plane_in[8 * stage : 8 * stage + 2 * nx], axis=0)
        line_src[stage] = row
        line_in[stage * nz + z] = row
        order = sorted(range(1, nz), key=lambda dz: -min(dz, nz - dz))
        for dz in order:
            remote(
                line_src.at[stage],
                line_in.at[stage * nz + z],
                line_s.at[stage],
                line_r.at[stage],
                peer(dz, 0, c),
            ).start()

    def line_total(stage):
        landed(line_in.at[pl.ds(stage * nz, nz - 1)], line_r.at[stage])
        return jnp.sum(line_in[stage * nz : (stage + 1) * nz], axis=0)

    plane_start(0)
    for dx in range(1, nx):
        remote(params.at[x], params.at[x], par_s, par_r, peer(0, dx, c)).start()

    for dx in (2, 1, 3, 0):
        for other in (0, 1):
            if dx == 0 and other == 0:
                continue
            to_col = c if other == 0 else 1 - c
            remote(
                lat.at[pl.ds(3 * to_col, 5)],
                r0.at[pl.ds(own_at + 1 - to_col, 5)],
                x0_s,
                x0_r.at[x * 2 + c],
                peer(0, dx, to_col),
            ).start()

    line_start(0)

    for dx in (0, 1, 3, 2):
        for other in (0, 1):
            from_x = lax.rem(x + dx, nx)
            from_c = c if other == 0 else 1 - c
            at = (from_x * 2 + from_c) * 6
            if not (dx == 0 and other == 0):
                landed(r0.at[pl.ds(nx * 12 + at + 1 - c, 5)], x0_r.at[from_x * 2 + from_c])
            for row, dz in ((0, 1), (2, nz - 1)):
                remote(
                    r0.at[pl.ds(nx * 12 + at, 5)],
                    r0.at[pl.ds(row * nx * 12 + at, 5)],
                    z0_s,
                    z0_r.at[(row // 2) * 8 + from_x * 2 + from_c],
                    peer(dz, 0, c),
                ).start()

    landed(params.at[pl.ds(0, nx - 1)], par_r)
    norm = affine(line_total(0), samples, params, 0, nx)

    def frames_of(row, block):
        at = (row * nx + block) * 12
        parts = []
        for col in range(2):
            v = r0[pl.ds(at + 6 * col, 5)].astype(F32)
            parts.append(v.reshape(10, 8, LANES))
        return jnp.concatenate(parts, axis=1)

    for row in (1, 0, 2):
        for block in range(nx):
            if row != 1:
                for col in range(2):
                    at = (row * nx + block) * 12 + 6 * col
                    landed(r0.at[pl.ds(at, 5)], z0_r.at[(row // 2) * 8 + block * 2 + col])
            scale, shift = norm[block]
            act0[row, :, :, block * LANES : (block + 1) * LANES] = activate(
                frames_of(row, block), scale, shift
            )

    @pl.when(z == 0)
    def _():
        act0[0] = jnp.zeros(act0.shape[1:], BF)

    @pl.when(z == nz - 1)
    def _():
        act0[2] = jnp.zeros(act0.shape[1:], BF)

    @pl.when(c == 0)
    def _():
        act0[:, 0:2] = jnp.zeros((3, 2, *act0.shape[2:]), BF)

    loads[0].wait()
    y = jnp.zeros((half * 16, 3 * LANES), F32)
    for dt in range(3):
        for di in range(3):
            y = y + dot(flat(act0[di, dt : dt + half]), taps(w0, dt, di))
    mixed = column_sum(y.reshape(half, 16, 3 * LANES))
    rest = frames_of(1, x)[2:10]
    value = (rest + mixed + c0[...].reshape(1, 1, LANES)).astype(BF)
    middle[...] = value
    plane_src[1] = packed_sums(flat(value.astype(F32)), x)
    plane_start(1)

    def spread(act):
        for j in range(half):
            for later in range(2):
                to_z = lax.rem(half * c + j + later, nz)
                fr = 1 - later
                for case in range(2):
                    if case == 0:
                        to_c = z // half
                        wanted = to_z >= 0
                    else:
                        to_c = 1 - z // half
                        wanted = (z == half - 1) | (z == half)
                    slot = z - half * to_c + 1
                    itself = (to_z == z) & (to_c == c)
                    act(j, fr, case, to_z, to_c, slot, wanted, itself)

    def a_copy(j, fr, case, to_z, to_c, slot):
        return remote(
            middle.at[j],
            x1.at[(x * 10 + slot) * 2 + fr],
            a_s.at[(j * 2 + fr) * 2 + case],
            a_r.at[slot * 2 + fr],
            {"seq": to_z, "ch": x, "col": to_c},
        )

    def a_start(j, fr, case, to_z, to_c, slot, wanted, itself):
        @pl.when(wanted & jnp.logical_not(itself))
        def _():
            a_copy(j, fr, case, to_z, to_c, slot).start()

        @pl.when(wanted & itself)
        def _():
            x1[(x * 10 + slot) * 2 + fr] = middle[j]

    def a_sent(j, fr, case, to_z, to_c, slot, wanted, itself):
        @pl.when(wanted & jnp.logical_not(itself))
        def _():
            a_copy(j, fr, case, to_z, to_c, slot).wait_send()

    spread(a_start)
    line_start(1)

    first = 1 - c
    for part in range(3):
        for i in range(3):
            slot = first + part * 3 + i
            source_row = half * c - 1 + slot
            for fr in range(2):
                source_c = lax.rem(z - 1 + fr + nz, nz) // half

                @pl.when(jnp.logical_not((source_row == z) & (source_c == c)))
                def _():
                    landed(x1.at[(x * 10 + slot) * 2 + fr], a_r.at[slot * 2 + fr])

        tiles = pl.ds((x * 10 + first + part * 3) * 2, 6)
        for dx in (2, 1, 3):
            remote(
                x1.at[tiles], x1.at[tiles], x1_s, x1_r.at[x * 3 + part], peer(0, dx, c)
            ).start()

    norm = affine(line_total(1), samples, params, 1, nx)
    for block in range(nx):
        @pl.when(block != x)
        def _():
            for part in range(3):
                landed(
                    x1.at[pl.ds((block * 10 + first + part * 3) * 2, 6)],
                    x1_r.at[block * 3 + part],
                )

        scale, shift = norm[block]
        v = x1[block * 20 : (block + 1) * 20].astype(F32).reshape(10, 2, 16, LANES)
        v = activate(v, scale, shift)
        for fr in range(2):
            act1[fr, :, :, block * LANES : (block + 1) * LANES] = v[:, fr]

    zero_row1 = jnp.zeros((2, 16, nx * LANES), BF)

    @pl.when(c == 0)
    def _():
        act1[:, 0] = zero_row1

    @pl.when(c == 1)
    def _():
        act1[:, 9] = zero_row1

    @pl.when(z == 0)
    def _():
        act1[0] = jnp.zeros(act1.shape[1:], BF)

    loads[1].wait()
    shared = jnp.zeros((half * 16, 3 * LANES), F32)
    apart = jnp.zeros((2 * half * 16, 3 * LANES), F32)
    for di in range(3):
        rows = act1[:, di : di + half]
        shared = shared + dot(flat(rows[0]), taps(w1, 0, di))
        shared = shared + dot(flat(rows[1]), taps(w1, 2, di))
    for di in range(3):
        apart = apart + dot(flat(act1[:, di : di + half]), taps(w1, 1, di))
    y = apart.reshape(2, half, 16, 3 * LANES) + shared.reshape(1, half, 16, 3 * LANES)
    mixed = column_sum(y.reshape(2 * half, 16, 3 * LANES))
    value = (mixed + c1[...].reshape(1, 1, LANES)).astype(BF)
    plane_src[2] = packed_sums(flat(value.astype(F32)), x)
    value = value.reshape(2, half, 16, LANES)
    for fr in range(2):
        for row in range(half):
            hidden[row * 2 + fr] = value[fr, row]
    plane_start(2)

    x2[pl.ds((x * 2 + 1) * 20 + 2, 2 * half)] = hidden[...]
    edge_at = pl.ds((2 * half - 2) * (1 - c), 2)
    edge_slot = pl.ds(18 * c, 2)
    for dz in (1, 0):
        for dx in (2, 1, 3, 0):
            if not (dz == 0 and dx == 0):
                remote(
                    hidden,
                    x2.at[pl.ds((x * 2 + 1 - dz) * 20 + 2, 2 * half)],
                    x2_s,
                    x2_r.at[(1 - dz) * nx + x],
                    peer(dz, dx, c),
                ).start()
            slot = pl.ds((x * 2 + 1 - dz) * 20 + 18 * c, 2)
            remote(
                hidden.at[edge_at], x2.at[slot], e2_s, e2_r.at[(1 - dz) * nx + x], peer(dz, dx, 1 - c)
            ).start()
    line_start(2)
    norm = affine(line_total(2), 2.0 * samples, params, 2, nx)

    for block in range(nx):
        for own_frames in (1, 0):
            sem = own_frames * nx + block
            at = (block * 2 + own_frames) * 20
            if own_frames:
                @pl.when(block != x)
                def _():
                    landed(x2.at[pl.ds(at + 2, 2 * half)], x2_r.at[sem])
            else:
                landed(x2.at[pl.ds(at + 2, 2 * half)], x2_r.at[sem])
            landed(x2.at[pl.ds(at + 18 * (1 - c), 2)], e2_r.at[sem])
            scale, shift = norm[block]
            v = x2[at : at + 20].astype(F32).reshape(10, 2, 16, LANES)
            v = activate(v, scale, shift)
            for fr in range(2):
                act2[2 * own_frames + fr, :, :, block * LANES : (block + 1) * LANES] = v[:, fr]

    zero_row2 = jnp.zeros((4, 16, nx * LANES), BF)

    @pl.when(c == 0)
    def _():
        act2[:, 0] = zero_row2

    @pl.when(c == 1)
    def _():
        act2[:, 9] = zero_row2

    @pl.when(z == 0)
    def _():
        act2[0:2] = jnp.zeros((2, *act2.shape[1:]), BF)

    loads[2].wait()
    y = jnp.zeros((2 * half * 16, 3 * LANES), F32)
    for dt in range(3):
        for di in range(3):
            y = y + dot(flat(act2[dt : dt + 2, di : di + half]), taps(w2, dt, di))
    mixed = column_sum(y.reshape(2 * half, 16, 3 * LANES)).reshape(2, half, 16, LANES)
    doubled = x1[pl.ds(x * 20 + 2, 2 * half)].astype(F32).reshape(half, 2, 16, LANES)[:, 1]
    final = doubled[None] + mixed + c2[...].reshape(1, 1, 1, LANES)

    sides = [
        final[:, :, 8 * side : 8 * side + 8].reshape(2, half // 2, 16, LANES).astype(BF)
        for side in range(2)
    ]

    @pl.when(c == 0)
    def _():
        give[...] = sides[1]
        out[:, pl.ds(0, half // 2)] = sides[0]

    @pl.when(c == 1)
    def _():
        give[...] = sides[0]
        out[:, pl.ds(half // 2, half // 2)] = sides[1]

    last = remote(give, take, o_s, o_r, peer(0, 0, 1 - c))
    last.start()

    for stage in range(3):
        landed(plane_in.at[pl.ds(8 * stage, 2 * nx - 1)], plane_s.at[stage])
        landed(line_in.at[pl.ds(stage * nz, nz - 1)], line_s.at[stage])
    landed(params.at[pl.ds(0, nx - 1)], par_s)
    landed(r0.at[pl.ds(0, 5 * (2 * nx - 1))], x0_s)
    landed(r0.at[pl.ds(0, 5 * 4 * nx)], z0_s)
    spread(a_sent)
    landed(x1.at[pl.ds(0, 3 * 3 * 6)], x1_s)
    landed(x2.at[pl.ds(0, 2 * half * (2 * nx - 1))], x2_s)
    landed(x2.at[pl.ds(0, 2 * 2 * nx)], e2_s)
    last.wait()

    @pl.when(c == 0)
    def _():
        out[:, pl.ds(half // 2, half // 2)] = take[...]

    @pl.when(c == 1)
    def _():
        out[:, pl.ds(0, half // 2)] = take[...]


def body(nz, nx, *args):
    latent = args[0]
    frames = latent.shape[0]
    half = nz // 2
    channels = nx * LANES
    operands = [latent.reshape(frames // 2, 16, LANES)]
    vmem = pl.BlockSpec(memory_space=pltpu.VMEM)
    specs = [vmem]
    for a in args[1:]:
        if a.ndim == 1:
            operands.append(a.reshape(1, LANES))
            specs.append(vmem)
        else:
            operands.append(a.reshape(27, channels, LANES))
            specs.append(pl.BlockSpec(memory_space=pl.ANY))
    weight = pltpu.VMEM((27, channels, LANES), BF)
    dma = pltpu.SemaphoreType.DMA
    result = pl.pallas_call(
        functools.partial(kernel, nz, nx),
        out_shape=jax.ShapeDtypeStruct((2, half, 16, LANES), BF),
        in_specs=specs,
        out_specs=vmem,
        scratch_shapes=[
            weight,
            weight,
            weight,
            pltpu.VMEM((nx, 8, LANES), F32),
            pltpu.VMEM((3 * nx * 2 * 6, 16, LANES), BF),
            pltpu.VMEM((nx * 10 * 2, 16, LANES), BF),
            pltpu.VMEM((nx * 2 * 10 * 2, 16, LANES), BF),
            pltpu.VMEM((3, half + 2, 16, channels), BF),
            pltpu.VMEM((2, half + 2, 16, channels), BF),
            pltpu.VMEM((4, half + 2, 16, channels), BF),
            pltpu.VMEM((half, 16, LANES), BF),
            pltpu.VMEM((2 * half, 16, LANES), BF),
            pltpu.VMEM((2, half // 2, 16, LANES), BF),
            pltpu.VMEM((2, half // 2, 16, LANES), BF),
            pltpu.VMEM((3, 1, LANES), F32),
            pltpu.VMEM((3 * 8, 1, LANES), F32),
            pltpu.VMEM((3, 1, LANES), F32),
            pltpu.VMEM((3 * nz, 1, LANES), F32),
            dma((3,)),
            dma,
            dma,
            dma((3,)),
            dma((3,)),
            dma((3,)),
            dma((3,)),
            dma,
            dma((2 * nx,)),
            dma,
            dma((4 * nx,)),
            dma((half * 4,)),
            dma((20,)),
            dma,
            dma((3 * nx,)),
            dma,
            dma((2 * nx,)),
            dma,
            dma((2 * nx,)),
            dma,
            dma,
        ],
        compiler_params=pltpu.CompilerParams(collective_id=0, has_side_effects=True),
    )(*operands)
    return result.reshape(2, nz, 8, LANES)


def solution(mesh):
    nz, nx = mesh.shape["seq"], mesh.shape["ch"]
    in_specs = (
        P("grp", "seq", "col", "ch"),
        *(P("ch"), P("ch"), P(None, None, None, None, "ch"), P("ch")) * 3,
    )
    out_specs = P(("grp", "seq"), None, "col", "ch")
    return jax.shard_map(
        functools.partial(body, nz, nx),
        mesh=mesh,
        in_specs=in_specs,
        out_specs=out_specs,
        check_vma=False,
    )
```

time: 211 us -> 73.7 us (0.35)
  blocking collectives: 133 us -> 0 us
  Pallas kernels: 0 us -> 72 us
  matrix products: 37.8 us -> 0 us
  starting transfers between devices: 25.1 us -> 0 us
  waiting for transfers between devices: 6.12 us -> 0 us
  other arithmetic: 3.7 us -> 0 us
  local copies, waits for them, and re-layouts: 4.03 us -> 1.47 us
    all_to_all x7 -> x0, blocking collectives: 133 us -> none  [the longest x6 115 us: sent_to_all(): return lax.all_to_all(copies, axis, split_axis=0, concat_axis=0, tiled=True)]
    pallas_call x0 -> x1, Pallas kernels: none -> 72 us  [body(): pl.pallas_call(functools.partial(kernel, nz, nx), out_shape=jax.ShapeDtyp...]
    dot_general x81 -> x0, matrix products: 37.8 us -> none  [channel_conv(): jnp.einsum('thwc,co->thwo', window, weight[tap_time, tap_row, tap_col], p...]
    ppermute x10 -> x0, starting transfers between devices: 25.1 us -> none  [the longest x4 12.8 us: extended_2(): after = lax.ppermute(first, axis, down)]
    ppermute x10 -> x0, waiting for transfers between devices: 6.12 us -> none  [the longest x2 2.62 us: shifted(): lax.ppermute(value, axis, [(source, source + steps) for source in range(f...]
    reshape x12 -> x0, local copies, waits for them, and re-layouts: 2.14 us -> none  [the longest x6 1.67 us: in_order(): blocks.reshape(*lengths[:dim], lengths[dim] * lengths[dim + 1], *lengths[...]
  transfers between devices with their start and end apart: 10 -> 0, of which waited for: 6 -> 0; matrix products, arithmetic and copies ran while one was open for 0% -> 0% of each run, Pallas kernels for 0% -> 0%
where the time goes in v1:
time: 73.7 us; the launch traced here: 73.5 us
  Pallas kernels  72 us (98%)
  local copies, waits for them, and re-layouts  1.47 us (2%)
    pallas_call x1, Pallas kernels, body(): pl.pallas_call(functools.partial(kernel, nz, nx), out_shape=jax.ShapeDtyp...  72 us
    unnamed x1, local copies, waits for them, and re-layouts  1.47 us

profile of v1, /device:TPU:33, one launch (start us, length us, event | category | flops | bytes accessed | tf_op | source)
XLA Modules:
  0.0 73.5 jit_solution(307708469484252045)
XLA Ops:
  0.0 72.0 %shard_map.127 = bf16[2,8,16,128]{3,2,1,0:T(8,128)(2,1)} custom-call(bf16[8,16,128]{2,1,0:T(8,128)(2,1)} %bitcast.18, f32[1,128]{1,0:T(1,128)} %bitcast.19, f32[1,128]{1,0:T(1,128)} %bitcast.20, bf16[27,512,128]{2,1,0:T(8,128)(2,1)} %bitcast.14, f32[1,128]{1,0:T(1,128)} %bitcast.21, f32[1,128]{1,0:T(1,128)} %bitcast.22, f32[1,128]{1,0:T(1,128)} %bitcast.23, ...), custom_call_target="tpu_custom_call" | custom-call | tf_op jit(solution)/shard_map/pallas_call | solution.py:543
  72.1 1.5 %copy.15 = bf16[2,16,8,128]{3,2,1,0:T(8,128)(2,1)} copy(bf16[2,16,8,128]{3,2,1,0:T(8,128)(2,1)} %bitcast.17) | data formatting | bytes 131072

commit v2 on v1

--- a/solution.py
+++ b/solution.py
@@ -93,7 +93,7 @@
 def kernel(
     nz,
     nx,
-    lat,
+    lat_hbm,
     g0,
     b0,
     w0_hbm,
@@ -107,6 +107,8 @@
     w2_hbm,
     c2,
     out,
+    lat,
+    vectors,
     w0,
     w1,
     w2,
@@ -125,6 +127,7 @@
     plane_in,
     line_src,
     line_in,
+    i_sem,
     w_sem,
     par_s,
     par_r,
@@ -142,6 +145,7 @@
     x1_r,
     x2_s,
     x2_r,
+    h2_r,
     e2_s,
     e2_r,
     o_s,
@@ -169,12 +173,15 @@
     def landed(ref, sem):
         pltpu.make_async_copy(ref, ref, sem).wait()
 
+    inputs = [pltpu.make_async_copy(lat_hbm, lat, i_sem.at[9])]
+    for i, ref in enumerate((g0, b0, g1, b1, g2, b2, c0, c1, c2)):
+        inputs.append(pltpu.make_async_copy(ref, vectors.at[i], i_sem.at[i]))
     loads = [
         pltpu.make_async_copy(a, b, w_sem.at[i])
         for i, (a, b) in enumerate(((w0_hbm, w0), (w1_hbm, w1), (w2_hbm, w2)))
     ]
-    for load in loads:
-        load.start()
+    for copy in inputs:
+        copy.start()
 
     barrier = pltpu.get_barrier_semaphore()
     greeted = []
@@ -190,9 +197,12 @@
     for dz, dx, col in greeted:
         pl.semaphore_signal(barrier, inc=1, device_id=peer(dz, dx, col), device_id_type=MESH)
 
-    mine = pl.multiple_of(x * 8, 8)
-    for i, ref in enumerate((g0, b0, g1, b1, g2, b2)):
-        params[x, i : i + 1, :] = ref[...]
+    for copy in inputs:
+        copy.wait()
+    for load in loads:
+        load.start()
+    for i in range(6):
+        params[x, i : i + 1, :] = vectors[i]
     own = lat[...].astype(F32)
     plane_src[0] = packed_sums(flat(own), x)
     own_at = ((nx + x) * 2 + c) * 6
@@ -310,80 +320,82 @@
             y = y + dot(flat(act0[di, dt : dt + half]), taps(w0, dt, di))
     mixed = column_sum(y.reshape(half, 16, 3 * LANES))
     rest = frames_of(1, x)[2:10]
-    value = (rest + mixed + c0[...].reshape(1, 1, LANES)).astype(BF)
+    value = (rest + mixed + vectors[6].reshape(1, 1, LANES)).astype(BF)
     middle[...] = value
     plane_src[1] = packed_sums(flat(value.astype(F32)), x)
     plane_start(1)
 
+    low, high = lax.rem(z - half * c + nz, nz), lax.rem(z - half * c - half + 1 + nz, nz)
+    ascending = jnp.minimum(low, nz - low) <= jnp.minimum(high, nz - high)
     def spread(act):
-        for j in range(half):
-            for later in range(2):
-                to_z = lax.rem(half * c + j + later, nz)
-                fr = 1 - later
-                for case in range(2):
-                    if case == 0:
-                        to_c = z // half
-                        wanted = to_z >= 0
-                    else:
-                        to_c = 1 - z // half
-                        wanted = (z == half - 1) | (z == half)
-                    slot = z - half * to_c + 1
-                    itself = (to_z == z) & (to_c == c)
-                    act(j, fr, case, to_z, to_c, slot, wanted, itself)
-
-    def a_copy(j, fr, case, to_z, to_c, slot):
-        return remote(
-            middle.at[j],
-            x1.at[(x * 10 + slot) * 2 + fr],
-            a_s.at[(j * 2 + fr) * 2 + case],
-            a_r.at[slot * 2 + fr],
-            {"seq": to_z, "ch": x, "col": to_c},
-        )
-
-    def a_start(j, fr, case, to_z, to_c, slot, wanted, itself):
+        for turn in range(half + 1):
+            j = jnp.where(ascending, half - turn, turn)
+            to_z = lax.rem(half * c + j, nz)
+            source = jnp.maximum(j - 1, 0)
+            tiles = 2 if 0 < turn < half else 1
+            fr = 0 if 0 < turn < half else jnp.where(j == 0, 1, 0)
+            for case in range(2):
+                if case == 0:
+                    to_c = z // half
+                    wanted = to_z >= 0
+                else:
+                    to_c = 1 - z // half
+                    wanted = (z == half - 1) | (z == half)
+                slot = z - half * to_c + 1
+                at = (x * 10 + slot) * 2 + fr
+                copy = remote(
+                    middle.at[pl.ds(source, tiles)],
+                    x1.at[pl.ds(at, tiles)],
+                    a_s.at[2 * turn + case],
+                    a_r.at[slot],
+                    {"seq": to_z, "ch": x, "col": to_c},
+                )
+                act(copy, source, tiles, at, wanted, (to_z == z) & (to_c == c))
+
+    def a_start(copy, source, tiles, at, wanted, itself):
         @pl.when(wanted & jnp.logical_not(itself))
         def _():
-            a_copy(j, fr, case, to_z, to_c, slot).start()
+            copy.start()
 
         @pl.when(wanted & itself)
         def _():
-            x1[(x * 10 + slot) * 2 + fr] = middle[j]
-
-    def a_sent(j, fr, case, to_z, to_c, slot, wanted, itself):
+            x1[pl.ds(at, tiles)] = middle[pl.ds(source, tiles)]
+
+    def a_sent(copy, source, tiles, at, wanted, itself):
         @pl.when(wanted & jnp.logical_not(itself))
         def _():
-            a_copy(j, fr, case, to_z, to_c, slot).wait_send()
+            copy.wait_send()
 
     spread(a_start)
     line_start(1)
 
     first = 1 - c
-    for part in range(3):
-        for i in range(3):
-            slot = first + part * 3 + i
-            source_row = half * c - 1 + slot
-            for fr in range(2):
-                source_c = lax.rem(z - 1 + fr + nz, nz) // half
-
-                @pl.when(jnp.logical_not((source_row == z) & (source_c == c)))
-                def _():
-                    landed(x1.at[(x * 10 + slot) * 2 + fr], a_r.at[slot * 2 + fr])
-
-        tiles = pl.ds((x * 10 + first + part * 3) * 2, 6)
+    previous_c = lax.rem(z - 1 + nz, nz) // half
+    for turn in range(9):
+        slot = first + jnp.where(ascending, turn, 8 - turn)
+        mine = half * c - 1 + slot == z
+        at = (x * 10 + slot) * 2
+        lost_old = mine & (previous_c == c)
+        lost_new = mine & (z // half == c)
+
+        @pl.when(jnp.logical_not(lost_old | lost_new))
+        def _():
+            landed(x1.at[pl.ds(at, 2)], a_r.at[slot])
+
+        @pl.when(lost_old ^ lost_new)
+        def _():
+            landed(x1.at[pl.ds(at, 1)], a_r.at[slot])
+
         for dx in (2, 1, 3):
             remote(
-                x1.at[tiles], x1.at[tiles], x1_s, x1_r.at[x * 3 + part], peer(0, dx, c)
+                x1.at[pl.ds(at, 2)], x1.at[pl.ds(at, 2)], x1_s, x1_r.at[x], peer(0, dx, c)
             ).start()
 
     norm = affine(line_total(1), samples, params, 1, nx)
     for block in range(nx):
         @pl.when(block != x)
         def _():
-            for part in range(3):
-                landed(
-                    x1.at[pl.ds((block * 10 + first + part * 3) * 2, 6)],
-                    x1_r.at[block * 3 + part],
-                )
+            landed(x1.at[pl.ds((block * 10 + first) * 2, 18)], x1_r.at[block])
 
         scale, shift = norm[block]
         v = x1[block * 20 : (block + 1) * 20].astype(F32).reshape(10, 2, 16, LANES)
@@ -416,7 +428,7 @@
         apart = apart + dot(flat(act1[:, di : di + half]), taps(w1, 1, di))
     y = apart.reshape(2, half, 16, 3 * LANES) + shared.reshape(1, half, 16, 3 * LANES)
     mixed = column_sum(y.reshape(2 * half, 16, 3 * LANES))
-    value = (mixed + c1[...].reshape(1, 1, LANES)).astype(BF)
+    value = (mixed + vectors[7].reshape(1, 1, LANES)).astype(BF)
     plane_src[2] = packed_sums(flat(value.astype(F32)), x)
     value = value.reshape(2, half, 16, LANES)
     for fr in range(2):
@@ -427,33 +439,40 @@
     x2[pl.ds((x * 2 + 1) * 20 + 2, 2 * half)] = hidden[...]
     edge_at = pl.ds((2 * half - 2) * (1 - c), 2)
     edge_slot = pl.ds(18 * c, 2)
+    def x2_block(block, own_frames):
+        return pl.ds((block * 2 + own_frames) * 20 + 2, 2 * half)
+
+    def history(part):
+        return x2.at[pl.ds(x * 40 + 2 + part * half, half)]
+
+    for part in range(2):
+        remote(
+            hidden.at[pl.ds(part * half, half)], history(part), x2_s, h2_r.at[part], peer(1, 0, c)
+        ).start()
+    for dx in (2, 1, 3):
+        remote(hidden, x2.at[x2_block(x, 1)], x2_s, x2_r.at[nx + x], peer(0, dx, c)).start()
     for dz in (1, 0):
         for dx in (2, 1, 3, 0):
-            if not (dz == 0 and dx == 0):
-                remote(
-                    hidden,
-                    x2.at[pl.ds((x * 2 + 1 - dz) * 20 + 2, 2 * half)],
-                    x2_s,
-                    x2_r.at[(1 - dz) * nx + x],
-                    peer(dz, dx, c),
-                ).start()
             slot = pl.ds((x * 2 + 1 - dz) * 20 + 18 * c, 2)
             remote(
                 hidden.at[edge_at], x2.at[slot], e2_s, e2_r.at[(1 - dz) * nx + x], peer(dz, dx, 1 - c)
             ).start()
     line_start(2)
+    for part in range(2):
+        landed(history(part), h2_r.at[part])
+        for dx in (2, 1, 3):
+            remote(history(part), history(part), x2_s, x2_r.at[x], peer(0, dx, c)).start()
     norm = affine(line_total(2), 2.0 * samples, params, 2, nx)
 
-    for block in range(nx):
-        for own_frames in (1, 0):
+    for own_frames in (1, 0):
+        for block in range(nx):
             sem = own_frames * nx + block
             at = (block * 2 + own_frames) * 20
-            if own_frames:
-                @pl.when(block != x)
-                def _():
-                    landed(x2.at[pl.ds(at + 2, 2 * half)], x2_r.at[sem])
-            else:
-                landed(x2.at[pl.ds(at + 2, 2 * half)], x2_r.at[sem])
+
+            @pl.when(block != x)
+            def _():
+                landed(x2.at[x2_block(block, own_frames)], x2_r.at[sem])
+
             landed(x2.at[pl.ds(at + 18 * (1 - c), 2)], e2_r.at[sem])
             scale, shift = norm[block]
             v = x2[at : at + 20].astype(F32).reshape(10, 2, 16, LANES)
@@ -482,7 +501,7 @@
             y = y + dot(flat(act2[dt : dt + 2, di : di + half]), taps(w2, dt, di))
     mixed = column_sum(y.reshape(2 * half, 16, 3 * LANES)).reshape(2, half, 16, LANES)
     doubled = x1[pl.ds(x * 20 + 2, 2 * half)].astype(F32).reshape(half, 2, 16, LANES)[:, 1]
-    final = doubled[None] + mixed + c2[...].reshape(1, 1, 1, LANES)
+    final = doubled[None] + mixed + vectors[8].reshape(1, 1, 1, LANES)
 
     sides = [
         final[:, :, 8 * side : 8 * side + 8].reshape(2, half // 2, 16, LANES).astype(BF)
@@ -529,23 +548,18 @@
     half = nz // 2
     channels = nx * LANES
     operands = [latent.reshape(frames // 2, 16, LANES)]
-    vmem = pl.BlockSpec(memory_space=pltpu.VMEM)
-    specs = [vmem]
     for a in args[1:]:
-        if a.ndim == 1:
-            operands.append(a.reshape(1, LANES))
-            specs.append(vmem)
-        else:
-            operands.append(a.reshape(27, channels, LANES))
-            specs.append(pl.BlockSpec(memory_space=pl.ANY))
+        operands.append(a.reshape((1, LANES) if a.ndim == 1 else (27, channels, LANES)))
     weight = pltpu.VMEM((27, channels, LANES), BF)
     dma = pltpu.SemaphoreType.DMA
     result = pl.pallas_call(
         functools.partial(kernel, nz, nx),
         out_shape=jax.ShapeDtypeStruct((2, half, 16, LANES), BF),
-        in_specs=specs,
-        out_specs=vmem,
+        in_specs=[pl.BlockSpec(memory_space=pl.ANY)] * len(operands),
+        out_specs=pl.BlockSpec(memory_space=pltpu.VMEM),
         scratch_shapes=[
+            pltpu.VMEM((frames // 2, 16, LANES), BF),
+            pltpu.VMEM((9, 1, LANES), F32),
             weight,
             weight,
             weight,
@@ -564,6 +578,7 @@
             pltpu.VMEM((3 * 8, 1, LANES), F32),
             pltpu.VMEM((3, 1, LANES), F32),
             pltpu.VMEM((3 * nz, 1, LANES), F32),
+            dma((10,)),
             dma((3,)),
             dma,
             dma,
@@ -575,12 +590,13 @@
             dma((2 * nx,)),
             dma,
             dma((4 * nx,)),
-            dma((half * 4,)),
-            dma((20,)),
-            dma,
-            dma((3 * nx,)),
+            dma((2 * half + 2,)),
+            dma((10,)),
+            dma,
+            dma((nx,)),
             dma,
             dma((2 * nx,)),
+            dma((2,)),
             dma,
             dma((2 * nx,)),
             dma,

time: 73.7 us -> 69.1 us (0.938)
  Pallas kernels: 72 us -> 67.4 us
    pallas_call x1, Pallas kernels: 72 us -> 67.4 us  [body(): pl.pallas_call(functools.partial(kernel, nz, nx), out_shape=jax.ShapeDtyp...]
where the time goes in v2:
time: 69.1 us; the launch traced here: 68.9 us
  Pallas kernels  67.4 us (98%)
  local copies, waits for them, and re-layouts  1.47 us (2%)
    pallas_call x1, Pallas kernels, body(): pl.pallas_call(functools.partial(kernel, nz, nx), out_shape=jax.ShapeDtyp...  67.4 us
    unnamed x1, local copies, waits for them, and re-layouts  1.47 us

profile of v2, /device:TPU:33, one launch (start us, length us, event | category | flops | bytes accessed | tf_op | source)
XLA Modules:
  0.0 68.9 jit_solution(1613319900610280654)
XLA Ops:
  0.0 67.4 %shard_map.127 = bf16[2,8,16,128]{3,2,1,0:T(8,128)(2,1)} custom-call(bf16[8,16,128]{2,1,0:T(8,128)(2,1)} %bitcast.18, f32[1,128]{1,0:T(1,128)} %bitcast.19, f32[1,128]{1,0:T(1,128)} %bitcast.20, bf16[27,512,128]{2,1,0:T(8,128)(2,1)} %bitcast.14, f32[1,128]{1,0:T(1,128)} %bitcast.21, f32[1,128]{1,0:T(1,128)} %bitcast.22, f32[1,128]{1,0:T(1,128)} %bitcast.23, ...), custom_call_target="tpu_custom_call" | custom-call | tf_op jit(solution)/shard_map/pallas_call | solution.py:555
  67.4 1.5 %copy.15 = bf16[2,16,8,128]{3,2,1,0:T(8,128)(2,1)} copy(bf16[2,16,8,128]{3,2,1,0:T(8,128)(2,1)} %bitcast.17) | data formatting | bytes 131072

commit v3 on v2

--- a/solution.py
+++ b/solution.py
@@ -184,15 +184,9 @@
         copy.start()
 
     barrier = pltpu.get_barrier_semaphore()
-    greeted = []
-    for dz in range(nz):
-        greeted.append((dz, 0, 1 - c))
-        if dz:
-            greeted.append((dz, 0, c))
-    for dz in (0, 1, nz - 1):
-        for dx in range(1, nx):
-            greeted.append((dz, dx, c))
-            greeted.append((dz, dx, 1 - c))
+    greeted = [(dz, 0, c) for dz in range(1, nz)] + [(0, 0, 1 - c)]
+    for dx in range(1, nx):
+        greeted += [(0, dx, c), (0, dx, 1 - c)]
     greeted.sort(key=lambda g: -min(g[0], nz - g[0]))
     for dz, dx, col in greeted:
         pl.semaphore_signal(barrier, inc=1, device_id=peer(dz, dx, col), device_id_type=MESH)
@@ -602,8 +596,8 @@
             dma,
             dma,
         ],
-        compiler_params=pltpu.CompilerParams(collective_id=0, has_side_effects=True),
-    )(*operands)
+        compiler_params=pltpu.CompilerParams(collective_id=0, has_side_effects=True, vmem_limit_bytes=50 * 2**20),
+    )(*[pltpu.with_memory_space_constraint(a, pltpu.HBM) for a in operands])
     return result.reshape(2, nz, 8, LANES)
 
 

time: 69.1 us -> 67.3 us (0.974)
  Pallas kernels: 67.4 us -> 66.5 us
  local copies, waits for them, and re-layouts: 1.47 us -> 0.63 us
    pallas_call x1, Pallas kernels: 67.4 us -> 66.5 us  [body(): pl.pallas_call(functools.partial(kernel, nz, nx), out_shape=jax.ShapeDtyp...]
    unnamed x1, local copies, waits for them, and re-layouts: 1.47 us -> 0.63 us
where the time goes in v3:
time: 67.3 us; the launch traced here: 67.1 us
  Pallas kernels  66.5 us (99%)
    pallas_call x1, Pallas kernels, body(): pl.pallas_call(functools.partial(kernel, nz, nx), out_shape=jax.ShapeDtyp...  66.5 us

profile of v3, /device:TPU:33, one launch (start us, length us, event | category | flops | bytes accessed | tf_op | source)
XLA Modules:
  0.0 67.1 jit_solution(9655530634948210692)
XLA Ops:
  0.0 66.5 %shard_map.127 = bf16[2,8,16,128]{3,2,1,0:T(8,128)(2,1)S(1)} custom-call(bf16[8,16,128]{2,1,0:T(8,128)(2,1)} %bitcast.18, f32[1,128]{1,0:T(1,128)} %bitcast.19, f32[1,128]{1,0:T(1,128)} %bitcast.20, bf16[27,512,128]{2,1,0:T(8,128)(2,1)} %bitcast.15, f32[1,128]{1,0:T(1,128)} %bitcast.21, f32[1,128]{1,0:T(1,128)} %bitcast.22, f32[1,128]{1,0:T(1,128)} %bitcast.23, ...), custom_call_target="tpu_custom_call" | custom-call | tf_op jit(solution)/shard_map/pallas_call | solution.py:549
  66.5 0.6 copy.15

commit v4 on v3

--- a/solution.py
+++ b/solution.py
@@ -127,10 +127,14 @@
     plane_in,
     line_src,
     line_in,
+    hub_in,
+    total_row,
     i_sem,
     w_sem,
     par_s,
     par_r,
+    hub_s,
+    hub_r,
     plane_s,
     plane_r,
     line_s,
@@ -183,13 +187,38 @@
     for copy in inputs:
         copy.start()
 
+    hub = 1
     barrier = pltpu.get_barrier_semaphore()
-    greeted = [(dz, 0, c) for dz in range(1, nz)] + [(0, 0, 1 - c)]
-    for dx in range(1, nx):
-        greeted += [(0, dx, c), (0, dx, 1 - c)]
-    greeted.sort(key=lambda g: -min(g[0], nz - g[0]))
-    for dz, dx, col in greeted:
+
+    def greet(dz, dx, col):
         pl.semaphore_signal(barrier, inc=1, device_id=peer(dz, dx, col), device_id_type=MESH)
+
+    greet(1, 0, c)
+    greet(nz - 1, 0, c)
+    for dx in range(nx):
+        greet(0, dx, 1 - c)
+        if dx:
+            greet(0, dx, c)
+
+    @pl.when(z == hub)
+    def _():
+        def greet_all(dz, carry):
+            for dx in range(nx):
+                greet(dz, dx, 1 - c)
+                if dx:
+                    greet(dz, dx, c)
+            return carry
+
+        lax.fori_loop(1, nz, greet_all, 0)
+
+        def greet_line(dz, carry):
+            greet(dz, 0, c)
+            return carry
+
+        lax.fori_loop(2, nz - 1, greet_line, 0)
+
+    near = (z == hub + 1) | (z == hub - 1)
+    awaited = 2 * nx + 1 + jnp.where(z == hub, 0, jnp.where(near, 2 * nx - 1, 2 * nx))
 
     for copy in inputs:
         copy.wait()
@@ -202,7 +231,60 @@
     own_at = ((nx + x) * 2 + c) * 6
     r0[pl.ds(own_at + 1 - c, 5)] = lat[pl.ds(3 * c, 5)]
 
-    pl.semaphore_wait(barrier, len(greeted))
+    pl.semaphore_wait(barrier, awaited)
+
+    def hub_start():
+        place = (z * nx + x) * 2 + c
+
+        @pl.when(z != hub)
+        def _():
+            for dx in (2, 1, 3, 0):
+                for col in (c, 1 - c):
+                    remote(
+                        plane_src.at[0],
+                        hub_in.at[place],
+                        hub_s,
+                        hub_r,
+                        {"seq": hub, "ch": lax.rem(x + dx, nx), "col": col},
+                    ).start()
+
+        @pl.when(z == hub)
+        def _():
+            hub_in[place] = plane_src[0]
+            for dx in (2, 1, 3, 0):
+                for col in (c, 1 - c):
+                    if dx == 0 and col is c:
+                        continue
+                    remote(
+                        plane_src.at[0],
+                        hub_in.at[place],
+                        plane_s.at[0],
+                        hub_r,
+                        {"seq": hub, "ch": lax.rem(x + dx, nx), "col": col},
+                    ).start()
+
+    def hub_run():
+        @pl.when(z == hub)
+        def _():
+            landed(hub_in.at[pl.ds(0, nz * nx * 2 - 1)], hub_r)
+            total_row[0] = jnp.sum(hub_in[...], axis=0)
+
+            def far_first(k, carry):
+                step = (k + 1) // 2
+                dz = half + step * (2 * lax.rem(k, 2) - 1)
+                remote(
+                    total_row.at[0], total_row.at[0], line_s.at[0], line_r.at[0], peer(dz, 0, c)
+                ).start()
+                return carry
+
+            lax.fori_loop(0, nz - 1, far_first, 0)
+
+    def hub_total():
+        @pl.when(z != hub)
+        def _():
+            landed(total_row.at[0], line_r.at[0])
+
+        return total_row[0]
 
     def plane_start(stage):
         place = 8 * stage + 2 * x + c
@@ -238,7 +320,7 @@
         landed(line_in.at[pl.ds(stage * nz, nz - 1)], line_r.at[stage])
         return jnp.sum(line_in[stage * nz : (stage + 1) * nz], axis=0)
 
-    plane_start(0)
+    hub_start()
     for dx in range(1, nx):
         remote(params.at[x], params.at[x], par_s, par_r, peer(0, dx, c)).start()
 
@@ -254,8 +336,6 @@
                 x0_r.at[x * 2 + c],
                 peer(0, dx, to_col),
             ).start()
-
-    line_start(0)
 
     for dx in (0, 1, 3, 2):
         for other in (0, 1):
@@ -273,8 +353,9 @@
                     peer(dz, 0, c),
                 ).start()
 
+    hub_run()
     landed(params.at[pl.ds(0, nx - 1)], par_r)
-    norm = affine(line_total(0), samples, params, 0, nx)
+    norm = affine(hub_total(), samples, params, 0, nx)
 
     def frames_of(row, block):
         at = (row * nx + block) * 12
@@ -315,58 +396,79 @@
     mixed = column_sum(y.reshape(half, 16, 3 * LANES))
     rest = frames_of(1, x)[2:10]
     value = (rest + mixed + vectors[6].reshape(1, 1, LANES)).astype(BF)
-    middle[...] = value
     plane_src[1] = packed_sums(flat(value.astype(F32)), x)
     plane_start(1)
-
-    low, high = lax.rem(z - half * c + nz, nz), lax.rem(z - half * c - half + 1 + nz, nz)
-    ascending = jnp.minimum(low, nz - low) <= jnp.minimum(high, nz - high)
-    def spread(act):
+    middle[...] = value
+
+    low, high = lax.rem(z - half * c + nz, nz), lax.rem(z - half * c - half + nz, nz)
+    low_near = jnp.minimum(low, nz - low) <= jnp.minimum(high, nz - high)
+
+    boundary = (z == half - 1) | (z == half)
+
+    def spread(act, case):
+        to_c = z // half if case == 0 else 1 - z // half
+        slot = z - half * to_c + 1
         for turn in range(half + 1):
-            j = jnp.where(ascending, half - turn, turn)
+            j = jnp.where(low_near, half - turn, turn)
             to_z = lax.rem(half * c + j, nz)
             source = jnp.maximum(j - 1, 0)
             tiles = 2 if 0 < turn < half else 1
             fr = 0 if 0 < turn < half else jnp.where(j == 0, 1, 0)
-            for case in range(2):
-                if case == 0:
-                    to_c = z // half
-                    wanted = to_z >= 0
-                else:
-                    to_c = 1 - z // half
-                    wanted = (z == half - 1) | (z == half)
-                slot = z - half * to_c + 1
-                at = (x * 10 + slot) * 2 + fr
-                copy = remote(
-                    middle.at[pl.ds(source, tiles)],
-                    x1.at[pl.ds(at, tiles)],
-                    a_s.at[2 * turn + case],
-                    a_r.at[slot],
-                    {"seq": to_z, "ch": x, "col": to_c},
-                )
-                act(copy, source, tiles, at, wanted, (to_z == z) & (to_c == c))
-
-    def a_start(copy, source, tiles, at, wanted, itself):
-        @pl.when(wanted & jnp.logical_not(itself))
+            at = (x * 10 + slot) * 2 + fr
+            copy = remote(
+                middle.at[pl.ds(source, tiles)],
+                x1.at[pl.ds(at, tiles)],
+                a_s.at[2 * turn + case],
+                a_r.at[slot],
+                {"seq": to_z, "ch": x, "col": to_c},
+            )
+            act(copy, source, tiles, at, (to_z == z) & (to_c == c))
+
+    def a_start(copy, source, tiles, at, itself):
+        @pl.when(jnp.logical_not(itself))
         def _():
             copy.start()
 
-        @pl.when(wanted & itself)
+    def a_keep(copy, source, tiles, at, itself):
+        @pl.when(itself)
         def _():
             x1[pl.ds(at, tiles)] = middle[pl.ds(source, tiles)]
 
-    def a_sent(copy, source, tiles, at, wanted, itself):
-        @pl.when(wanted & jnp.logical_not(itself))
+    def a_sent(copy, source, tiles, at, itself):
+        @pl.when(jnp.logical_not(itself))
         def _():
             copy.wait_send()
 
-    spread(a_start)
-    line_start(1)
+    spread(a_start, 0)
+
+    @pl.when(boundary)
+    def _():
+        spread(a_start, 1)
+        spread(a_keep, 1)
+
+    @pl.when(z // half == c)
+    def _():
+        spread(a_keep, 0)
 
     first = 1 - c
     previous_c = lax.rem(z - 1 + nz, nz) // half
+    whole_own = (previous_c == c) & (z // half == c)
+
+    def row_over_ch(slot):
+        tiles = pl.ds((x * 10 + slot) * 2, 2)
+        for dx in (2, 1, 3):
+            remote(
+                x1.at[tiles], x1.at[tiles], x1_s, x1_r.at[x], peer(0, dx, c)
+            ).start()
+
+    @pl.when(whole_own)
+    def _():
+        row_over_ch(z - half * c + 1)
+
+    line_start(1)
+
     for turn in range(9):
-        slot = first + jnp.where(ascending, turn, 8 - turn)
+        slot = first + jnp.where(c == 0, turn, 8 - turn)
         mine = half * c - 1 + slot == z
         at = (x * 10 + slot) * 2
         lost_old = mine & (previous_c == c)
@@ -380,10 +482,9 @@
         def _():
             landed(x1.at[pl.ds(at, 1)], a_r.at[slot])
 
-        for dx in (2, 1, 3):
-            remote(
-                x1.at[pl.ds(at, 2)], x1.at[pl.ds(at, 2)], x1_s, x1_r.at[x], peer(0, dx, c)
-            ).start()
+        @pl.when(jnp.logical_not(mine & whole_own))
+        def _():
+            row_over_ch(slot)
 
     norm = affine(line_total(1), samples, params, 1, nx)
     for block in range(nx):
@@ -424,13 +525,12 @@
     mixed = column_sum(y.reshape(2 * half, 16, 3 * LANES))
     value = (mixed + vectors[7].reshape(1, 1, LANES)).astype(BF)
     plane_src[2] = packed_sums(flat(value.astype(F32)), x)
+    plane_start(2)
     value = value.reshape(2, half, 16, LANES)
     for fr in range(2):
         for row in range(half):
             hidden[row * 2 + fr] = value[fr, row]
-    plane_start(2)
-
-    x2[pl.ds((x * 2 + 1) * 20 + 2, 2 * half)] = hidden[...]
+
     edge_at = pl.ds((2 * half - 2) * (1 - c), 2)
     edge_slot = pl.ds(18 * c, 2)
     def x2_block(block, own_frames):
@@ -451,6 +551,7 @@
             remote(
                 hidden.at[edge_at], x2.at[slot], e2_s, e2_r.at[(1 - dz) * nx + x], peer(dz, dx, 1 - c)
             ).start()
+    x2[pl.ds((x * 2 + 1) * 20 + 2, 2 * half)] = hidden[...]
     line_start(2)
     for part in range(2):
         landed(history(part), h2_r.at[part])
@@ -515,13 +616,27 @@
     last = remote(give, take, o_s, o_r, peer(0, 0, 1 - c))
     last.start()
 
-    for stage in range(3):
+    @pl.when(z != hub)
+    def _():
+        landed(hub_in.at[pl.ds(0, 2 * nx)], hub_s)
+
+    @pl.when(z == hub)
+    def _():
+        landed(hub_in.at[pl.ds(0, 2 * nx - 1)], plane_s.at[0])
+        landed(hub_in.at[pl.ds(0, nz - 1)], line_s.at[0])
+
+    for stage in (1, 2):
         landed(plane_in.at[pl.ds(8 * stage, 2 * nx - 1)], plane_s.at[stage])
         landed(line_in.at[pl.ds(stage * nz, nz - 1)], line_s.at[stage])
     landed(params.at[pl.ds(0, nx - 1)], par_s)
     landed(r0.at[pl.ds(0, 5 * (2 * nx - 1))], x0_s)
     landed(r0.at[pl.ds(0, 5 * 4 * nx)], z0_s)
-    spread(a_sent)
+    spread(a_sent, 0)
+
+    @pl.when(boundary)
+    def _():
+        spread(a_sent, 1)
+
     landed(x1.at[pl.ds(0, 3 * 3 * 6)], x1_s)
     landed(x2.at[pl.ds(0, 2 * half * (2 * nx - 1))], x2_s)
     landed(x2.at[pl.ds(0, 2 * 2 * nx)], e2_s)
@@ -572,8 +687,12 @@
             pltpu.VMEM((3 * 8, 1, LANES), F32),
             pltpu.VMEM((3, 1, LANES), F32),
             pltpu.VMEM((3 * nz, 1, LANES), F32),
+            pltpu.VMEM((nz * nx * 2, 1, LANES), F32),
+            pltpu.VMEM((1, 1, LANES), F32),
             dma((10,)),
             dma((3,)),
+            dma,
+            dma,
             dma,
             dma,
             dma((3,)),

time: 67.3 us -> 64.7 us (0.961)
  Pallas kernels: 66.5 us -> 63.9 us
    pallas_call x1, Pallas kernels: 66.5 us -> 63.9 us  [body(): pl.pallas_call(functools.partial(kernel, nz, nx), out_shape=jax.ShapeDtyp...]
where the time goes in v4:
time: 64.7 us; the launch traced here: 64.5 us
  Pallas kernels  63.9 us (99%)
    pallas_call x1, Pallas kernels, body(): pl.pallas_call(functools.partial(kernel, nz, nx), out_shape=jax.ShapeDtyp...  63.9 us

profile of v4, /device:TPU:33, one launch (start us, length us, event | category | flops | bytes accessed | tf_op | source)
XLA Modules:
  0.0 64.5 jit_solution(4385971654840287857)
XLA Ops:
  0.0 63.9 %shard_map.127 = bf16[2,8,16,128]{3,2,1,0:T(8,128)(2,1)S(1)} custom-call(bf16[8,16,128]{2,1,0:T(8,128)(2,1)} %bitcast.18, f32[1,128]{1,0:T(1,128)} %bitcast.19, f32[1,128]{1,0:T(1,128)} %bitcast.20, bf16[27,512,128]{2,1,0:T(8,128)(2,1)} %bitcast.15, f32[1,128]{1,0:T(1,128)} %bitcast.21, f32[1,128]{1,0:T(1,128)} %bitcast.22, f32[1,128]{1,0:T(1,128)} %bitcast.23, ...), custom_call_target="tpu_custom_call" | custom-call | tf_op jit(solution)/shard_map/pallas_call | solution.py:664
  63.9 0.6 copy.15

commit v5 on v4

--- a/solution.py
+++ b/solution.py
@@ -77,9 +77,12 @@
     return left + mid + right
 
 
-def taps(weight, dt, di):
+def taps(weight, dt, di, blocks):
     base = dt * 9 + di * 3
-    return jnp.concatenate([weight[base + dj] for dj in range(3)], axis=1)
+    rows = [pl.ds(pl.multiple_of(block * LANES, LANES), LANES) for block in blocks]
+    return jnp.concatenate(
+        [jnp.concatenate([weight[base + dj, r] for r in rows], axis=0) for dj in range(3)], axis=1
+    )
 
 
 def dot(a, b):
@@ -119,6 +122,7 @@
     act0,
     act1,
     act2,
+    scales,
     middle,
     hidden,
     give,
@@ -337,6 +341,16 @@
                 peer(0, dx, to_col),
             ).start()
 
+    @pl.when(c == 0)
+    def _():
+        for i in range(2 * nx):
+            r0[nx * 12 + 6 * i] = jnp.zeros((16, LANES), BF)
+
+    for block in range(nx):
+        x1[pl.ds((block * 10 + 9 * c) * 2, 2)] = jnp.zeros((2, 16, LANES), BF)
+    for block in range(2 * nx):
+        x2[pl.ds((block * 10 + 9 * c) * 2, 2)] = jnp.zeros((2, 16, LANES), BF)
+
     for dx in (0, 1, 3, 2):
         for other in (0, 1):
             from_x = lax.rem(x + dx, nx)
@@ -365,34 +379,36 @@
             parts.append(v.reshape(10, 8, LANES))
         return jnp.concatenate(parts, axis=1)
 
-    for row in (1, 0, 2):
+    for row in (0, 2):
         for block in range(nx):
-            if row != 1:
-                for col in range(2):
-                    at = (row * nx + block) * 12 + 6 * col
-                    landed(r0.at[pl.ds(at, 5)], z0_r.at[(row // 2) * 8 + block * 2 + col])
-            scale, shift = norm[block]
-            act0[row, :, :, block * LANES : (block + 1) * LANES] = activate(
-                frames_of(row, block), scale, shift
-            )
-
-    @pl.when(z == 0)
-    def _():
-        act0[0] = jnp.zeros(act0.shape[1:], BF)
-
-    @pl.when(z == nz - 1)
-    def _():
-        act0[2] = jnp.zeros(act0.shape[1:], BF)
-
-    @pl.when(c == 0)
-    def _():
-        act0[:, 0:2] = jnp.zeros((3, 2, *act0.shape[2:]), BF)
-
+            for col in range(2):
+                at = (row * nx + block) * 12 + 6 * col
+                landed(r0.at[pl.ds(at, 5)], z0_r.at[(row // 2) * 8 + block * 2 + col])
     loads[0].wait()
+
+    def inside(condition):
+        return jnp.where(condition, 1.0, 0.0).astype(F32)
+
+    in_row = (inside(z > 0), 1.0, inside(z < nz - 1))
+    in_core = (inside(c > 0), inside(c < 1))
+    in_time = inside(z > 0)
+
     y = jnp.zeros((half * 16, 3 * LANES), F32)
-    for dt in range(3):
+    for pair in range(nx // 2):
+        for k in range(2):
+            scale, shift = norm[2 * pair + k]
+            lanes = slice(k * LANES, (k + 1) * LANES)
+            for row in range(3):
+                v = frames_of(row, 2 * pair + k)
+                keep = in_row[row] * in_core[0]
+                act0[pair, row, 0:2, :, lanes] = activate(v[0:2], scale * keep, shift * keep)
+                keep = in_row[row]
+                act0[pair, row, 2:, :, lanes] = activate(v[2:], scale * keep, shift * keep)
         for di in range(3):
-            y = y + dot(flat(act0[di, dt : dt + half]), taps(w0, dt, di))
+            for dt in range(3):
+                y = y + dot(
+                    flat(act0[pair, di, dt : dt + half]), taps(w0, dt, di, (2 * pair, 2 * pair + 1))
+                )
     mixed = column_sum(y.reshape(half, 16, 3 * LANES))
     rest = frames_of(1, x)[2:10]
     value = (rest + mixed + vectors[6].reshape(1, 1, LANES)).astype(BF)
@@ -488,39 +504,32 @@
 
     norm = affine(line_total(1), samples, params, 1, nx)
     for block in range(nx):
-        @pl.when(block != x)
-        def _():
-            landed(x1.at[pl.ds((block * 10 + first) * 2, 18)], x1_r.at[block])
-
-        scale, shift = norm[block]
-        v = x1[block * 20 : (block + 1) * 20].astype(F32).reshape(10, 2, 16, LANES)
-        v = activate(v, scale, shift)
-        for fr in range(2):
-            act1[fr, :, :, block * LANES : (block + 1) * LANES] = v[:, fr]
-
-    zero_row1 = jnp.zeros((2, 16, nx * LANES), BF)
-
-    @pl.when(c == 0)
-    def _():
-        act1[:, 0] = zero_row1
-
-    @pl.when(c == 1)
-    def _():
-        act1[:, 9] = zero_row1
-
-    @pl.when(z == 0)
-    def _():
-        act1[0] = jnp.zeros(act1.shape[1:], BF)
-
+        scales[2 * block] = norm[block][0]
+        scales[2 * block + 1] = norm[block][1]
     loads[1].wait()
+    bands = ((0, 1, in_core[0]), (1, half + 1, 1.0), (half + 1, half + 2, in_core[1]))
+
     shared = jnp.zeros((half * 16, 3 * LANES), F32)
     apart = jnp.zeros((2 * half * 16, 3 * LANES), F32)
-    for di in range(3):
-        rows = act1[:, di : di + half]
-        shared = shared + dot(flat(rows[0]), taps(w1, 0, di))
-        shared = shared + dot(flat(rows[1]), taps(w1, 2, di))
-    for di in range(3):
-        apart = apart + dot(flat(act1[:, di : di + half]), taps(w1, 1, di))
+    for pair, steps in enumerate(((0, 1), (3, 2))):
+        blocks = [lax.rem(x + step, nx) for step in steps]
+        for block, step in zip(blocks, steps):
+            if step:
+                landed(x1.at[pl.ds((block * 10 + first) * 2, 18)], x1_r.at[block])
+        for k, block in enumerate(blocks):
+            scale, shift = scales[2 * block], scales[2 * block + 1]
+            v = x1[pl.ds(block * 20, 20)].astype(F32).reshape(half + 2, 2, 16, LANES)
+            for fr in range(2):
+                for lo, hi, keep in bands:
+                    keep = keep * in_time if fr == 0 else keep
+                    act1[pair, fr, lo:hi, :, k * LANES : (k + 1) * LANES] = activate(
+                        v[lo:hi, fr], scale * keep, shift * keep
+                    )
+        for di in range(3):
+            rows = act1[pair, :, di : di + half]
+            shared = shared + dot(flat(rows[0]), taps(w1, 0, di, blocks))
+            shared = shared + dot(flat(rows[1]), taps(w1, 2, di, blocks))
+            apart = apart + dot(flat(rows), taps(w1, 1, di, blocks))
     y = apart.reshape(2, half, 16, 3 * LANES) + shared.reshape(1, half, 16, 3 * LANES)
     mixed = column_sum(y.reshape(2 * half, 16, 3 * LANES))
     value = (mixed + vectors[7].reshape(1, 1, LANES)).astype(BF)
@@ -569,31 +578,27 @@
                 landed(x2.at[x2_block(block, own_frames)], x2_r.at[sem])
 
             landed(x2.at[pl.ds(at + 18 * (1 - c), 2)], e2_r.at[sem])
+    loads[2].wait()
+
+    y = jnp.zeros((2 * half * 16, 3 * LANES), F32)
+    for pair in range(nx // 2):
+        for k in range(2):
+            block = 2 * pair + k
             scale, shift = norm[block]
-            v = x2[at : at + 20].astype(F32).reshape(10, 2, 16, LANES)
-            v = activate(v, scale, shift)
-            for fr in range(2):
-                act2[2 * own_frames + fr, :, :, block * LANES : (block + 1) * LANES] = v[:, fr]
-
-    zero_row2 = jnp.zeros((4, 16, nx * LANES), BF)
-
-    @pl.when(c == 0)
-    def _():
-        act2[:, 0] = zero_row2
-
-    @pl.when(c == 1)
-    def _():
-        act2[:, 9] = zero_row2
-
-    @pl.when(z == 0)
-    def _():
-        act2[0:2] = jnp.zeros((2, *act2.shape[1:]), BF)
-
-    loads[2].wait()
-    y = jnp.zeros((2 * half * 16, 3 * LANES), F32)
-    for dt in range(3):
+            for own_frames in range(2):
+                at = (block * 2 + own_frames) * 20
+                v = x2[at : at + 20].astype(F32).reshape(half + 2, 2, 16, LANES)
+                for lo, hi, keep in bands:
+                    keep = keep if own_frames else keep * in_time
+                    part = activate(v[lo:hi], scale * keep, shift * keep)
+                    for fr in range(2):
+                        act2[pair, 2 * own_frames + fr, lo:hi, :, k * LANES : (k + 1) * LANES] = part[:, fr]
         for di in range(3):
-            y = y + dot(flat(act2[dt : dt + 2, di : di + half]), taps(w2, dt, di))
+            for dt in range(3):
+                y = y + dot(
+                    flat(act2[pair, dt : dt + 2, di : di + half]),
+                    taps(w2, dt, di, (2 * pair, 2 * pair + 1)),
+                )
     mixed = column_sum(y.reshape(2 * half, 16, 3 * LANES)).reshape(2, half, 16, LANES)
     doubled = x1[pl.ds(x * 20 + 2, 2 * half)].astype(F32).reshape(half, 2, 16, LANES)[:, 1]
     final = doubled[None] + mixed + vectors[8].reshape(1, 1, 1, LANES)
@@ -676,9 +681,10 @@
             pltpu.VMEM((3 * nx * 2 * 6, 16, LANES), BF),
             pltpu.VMEM((nx * 10 * 2, 16, LANES), BF),
             pltpu.VMEM((nx * 2 * 10 * 2, 16, LANES), BF),
-            pltpu.VMEM((3, half + 2, 16, channels), BF),
-            pltpu.VMEM((2, half + 2, 16, channels), BF),
-            pltpu.VMEM((4, half + 2, 16, channels), BF),
+            pltpu.VMEM((nx // 2, 3, half + 2, 16, 2 * LANES), BF),
+            pltpu.VMEM((nx // 2, 2, half + 2, 16, 2 * LANES), BF),
+            pltpu.VMEM((nx // 2, 4, half + 2, 16, 2 * LANES), BF),
+            pltpu.VMEM((2 * nx, 1, LANES), F32),
             pltpu.VMEM((half, 16, LANES), BF),
             pltpu.VMEM((2 * half, 16, LANES), BF),
             pltpu.VMEM((2, half // 2, 16, LANES), BF),

time: 64.7 us -> 64.3 us (level)
  no operation moved by 1% of the time
where the time goes in v5:
time: 64.3 us; the launch traced here: 64.1 us
  Pallas kernels  63.5 us (99%)
    pallas_call x1, Pallas kernels, body(): pl.pallas_call(functools.partial(kernel, nz, nx), out_shape=jax.ShapeDtyp...  63.5 us

profile of v5, /device:TPU:33, one launch (start us, length us, event | category | flops | bytes accessed | tf_op | source)
XLA Modules:
  0.0 64.1 jit_solution(2147148466926376730)
XLA Ops:
  0.0 63.5 %shard_map.127 = bf16[2,8,16,128]{3,2,1,0:T(8,128)(2,1)S(1)} custom-call(bf16[8,16,128]{2,1,0:T(8,128)(2,1)} %bitcast.18, f32[1,128]{1,0:T(1,128)} %bitcast.19, f32[1,128]{1,0:T(1,128)} %bitcast.20, bf16[27,512,128]{2,1,0:T(8,128)(2,1)} %bitcast.15, f32[1,128]{1,0:T(1,128)} %bitcast.21, f32[1,128]{1,0:T(1,128)} %bitcast.22, f32[1,128]{1,0:T(1,128)} %bitcast.23, ...), custom_call_target="tpu_custom_call" | custom-call | tf_op jit(solution)/shard_map/pallas_call | solution.py:669
  63.5 0.6 copy.15

commit v6 on v5

--- a/solution.py
+++ b/solution.py
@@ -133,6 +133,7 @@
     line_in,
     hub_in,
     total_row,
+    far_in,
     i_sem,
     w_sem,
     par_s,
@@ -143,6 +144,8 @@
     plane_r,
     line_s,
     line_r,
+    far_s,
+    far_r,
     x0_s,
     x0_r,
     z0_s,
@@ -197,8 +200,14 @@
     def greet(dz, dx, col):
         pl.semaphore_signal(barrier, inc=1, device_id=peer(dz, dx, col), device_id_type=MESH)
 
-    greet(1, 0, c)
-    greet(nz - 1, 0, c)
+    @pl.when(z < nz - 1)
+    def _():
+        greet(1, 0, c)
+
+    @pl.when(z > 0)
+    def _():
+        greet(nz - 1, 0, c)
+
     for dx in range(nx):
         greet(0, dx, 1 - c)
         if dx:
@@ -223,6 +232,7 @@
 
     near = (z == hub + 1) | (z == hub - 1)
     awaited = 2 * nx + 1 + jnp.where(z == hub, 0, jnp.where(near, 2 * nx - 1, 2 * nx))
+    awaited = awaited - jnp.where((z == 0) | (z == nz - 1), 1, 0)
 
     for copy in inputs:
         copy.wait()
@@ -305,24 +315,46 @@
                     peer(0, dx, c if other == 0 else 1 - c),
                 ).start()
 
+    across = (half, half - 1, half + 1)
+
+    def far_start():
+        for k, dz in enumerate(across):
+            for dx in (2, 1, 3, 0):
+                for col in (c, 1 - c):
+                    remote(
+                        plane_src.at[2],
+                        far_in.at[8 * k + 2 * x + c],
+                        far_s,
+                        far_r,
+                        peer(dz, dx, col),
+                    ).start()
+
+    def line_steps(stage):
+        steps = sorted(range(1, nz), key=lambda dz: -min(dz, nz - dz))
+        return [dz for dz in steps if stage == 1 or dz not in across]
+
     def line_start(stage):
         landed(plane_in.at[pl.ds(8 * stage, 2 * nx - 1)], plane_r.at[stage])
         row = jnp.sum(plane_in[8 * stage : 8 * stage + 2 * nx], axis=0)
         line_src[stage] = row
-        line_in[stage * nz + z] = row
-        order = sorted(range(1, nz), key=lambda dz: -min(dz, nz - dz))
-        for dz in order:
+        line_in[stage * nz] = row
+        for dz in line_steps(stage):
             remote(
                 line_src.at[stage],
-                line_in.at[stage * nz + z],
+                line_in.at[stage * nz + nz - dz],
                 line_s.at[stage],
                 line_r.at[stage],
                 peer(dz, 0, c),
             ).start()
 
     def line_total(stage):
-        landed(line_in.at[pl.ds(stage * nz, nz - 1)], line_r.at[stage])
-        return jnp.sum(line_in[stage * nz : (stage + 1) * nz], axis=0)
+        landed(line_in.at[pl.ds(stage * nz, len(line_steps(stage)))], line_r.at[stage])
+        if stage == 1:
+            return jnp.sum(line_in[nz : 2 * nz], axis=0)
+        landed(far_in, far_r)
+        total = jnp.sum(line_in[stage * nz : stage * nz + half - 1], axis=0)
+        total = total + jnp.sum(line_in[stage * nz + half + 2 : (stage + 1) * nz], axis=0)
+        return total + jnp.sum(far_in[...], axis=0)
 
     hub_start()
     for dx in range(1, nx):
@@ -346,6 +378,16 @@
         for i in range(2 * nx):
             r0[nx * 12 + 6 * i] = jnp.zeros((16, LANES), BF)
 
+    for row, outside in ((0, z == 0), (2, z == nz - 1)):
+        @pl.when(outside)
+        def _():
+            r0[row * nx * 12 : (row + 1) * nx * 12] = jnp.zeros((nx * 12, 16, LANES), BF)
+
+    @pl.when(z == 0)
+    def _():
+        for block in range(nx):
+            x2[block * 40 : block * 40 + 20] = jnp.zeros((20, 16, LANES), BF)
+
     for block in range(nx):
         x1[pl.ds((block * 10 + 9 * c) * 2, 2)] = jnp.zeros((2, 16, LANES), BF)
     for block in range(2 * nx):
@@ -358,14 +400,17 @@
             at = (from_x * 2 + from_c) * 6
             if not (dx == 0 and other == 0):
                 landed(r0.at[pl.ds(nx * 12 + at + 1 - c, 5)], x0_r.at[from_x * 2 + from_c])
-            for row, dz in ((0, 1), (2, nz - 1)):
-                remote(
-                    r0.at[pl.ds(nx * 12 + at, 5)],
-                    r0.at[pl.ds(row * nx * 12 + at, 5)],
-                    z0_s,
-                    z0_r.at[(row // 2) * 8 + from_x * 2 + from_c],
-                    peer(dz, 0, c),
-                ).start()
+            for row, dz, there in ((0, 1, z < nz - 1), (2, nz - 1, z > 0)):
+                @pl.when(there)
+                def _():
+                    remote(
+                        r0.at[pl.ds(nx * 12 + at, 5)],
+                        r0.at[pl.ds(row * nx * 12 + at, 5)],
+                        z0_s.at[row // 2],
+                        z0_r.at[(row // 2) * 8 + from_x * 2 + from_c],
+                        peer(dz, 0, c),
+                    ).start()
+
 
     hub_run()
     landed(params.at[pl.ds(0, nx - 1)], par_r)
@@ -379,11 +424,14 @@
             parts.append(v.reshape(10, 8, LANES))
         return jnp.concatenate(parts, axis=1)
 
-    for row in (0, 2):
-        for block in range(nx):
-            for col in range(2):
-                at = (row * nx + block) * 12 + 6 * col
-                landed(r0.at[pl.ds(at, 5)], z0_r.at[(row // 2) * 8 + block * 2 + col])
+    for row, there in ((0, z > 0), (2, z < nz - 1)):
+        @pl.when(there)
+        def _():
+            for block in range(nx):
+                for col in range(2):
+                    at = (row * nx + block) * 12 + 6 * col
+                    landed(r0.at[pl.ds(at, 5)], z0_r.at[(row // 2) * 8 + block * 2 + col])
+
     loads[0].wait()
 
     def inside(condition):
@@ -535,6 +583,7 @@
     value = (mixed + vectors[7].reshape(1, 1, LANES)).astype(BF)
     plane_src[2] = packed_sums(flat(value.astype(F32)), x)
     plane_start(2)
+    far_start()
     value = value.reshape(2, half, 16, LANES)
     for fr in range(2):
         for row in range(half):
@@ -548,27 +597,54 @@
     def history(part):
         return x2.at[pl.ds(x * 40 + 2 + part * half, half)]
 
-    for part in range(2):
-        remote(
-            hidden.at[pl.ds(part * half, half)], history(part), x2_s, h2_r.at[part], peer(1, 0, c)
-        ).start()
-    for dx in (2, 1, 3):
-        remote(hidden, x2.at[x2_block(x, 1)], x2_s, x2_r.at[nx + x], peer(0, dx, c)).start()
-    for dz in (1, 0):
+    has_next, has_past = z < nz - 1, z > 0
+
+    def edges(dz):
         for dx in (2, 1, 3, 0):
             slot = pl.ds((x * 2 + 1 - dz) * 20 + 18 * c, 2)
             remote(
-                hidden.at[edge_at], x2.at[slot], e2_s, e2_r.at[(1 - dz) * nx + x], peer(dz, dx, 1 - c)
+                hidden.at[edge_at],
+                x2.at[slot],
+                e2_s.at[dz],
+                e2_r.at[(1 - dz) * nx + x],
+                peer(dz, dx, 1 - c),
             ).start()
+
+    @pl.when(has_next)
+    def _():
+        for part in range(2):
+            remote(
+                hidden.at[pl.ds(part * half, half)],
+                history(part),
+                x2_s.at[1],
+                h2_r.at[part],
+                peer(1, 0, c),
+            ).start()
+
+    for dx in (2, 1, 3):
+        remote(
+            hidden, x2.at[x2_block(x, 1)], x2_s.at[0], x2_r.at[nx + x], peer(0, dx, c)
+        ).start()
+    edges(0)
+
+    @pl.when(has_next)
+    def _():
+        edges(1)
+
     x2[pl.ds((x * 2 + 1) * 20 + 2, 2 * half)] = hidden[...]
     line_start(2)
-    for part in range(2):
-        landed(history(part), h2_r.at[part])
-        for dx in (2, 1, 3):
-            remote(history(part), history(part), x2_s, x2_r.at[x], peer(0, dx, c)).start()
+    @pl.when(has_past)
+    def _():
+        for part in range(2):
+            landed(history(part), h2_r.at[part])
+            for dx in (2, 1, 3):
+                remote(
+                    history(part), history(part), x2_s.at[2], x2_r.at[x], peer(0, dx, c)
+                ).start()
+
     norm = affine(line_total(2), 2.0 * samples, params, 2, nx)
 
-    for own_frames in (1, 0):
+    def arrived(own_frames):
         for block in range(nx):
             sem = own_frames * nx + block
             at = (block * 2 + own_frames) * 20
@@ -578,6 +654,13 @@
                 landed(x2.at[x2_block(block, own_frames)], x2_r.at[sem])
 
             landed(x2.at[pl.ds(at + 18 * (1 - c), 2)], e2_r.at[sem])
+
+    arrived(1)
+
+    @pl.when(has_past)
+    def _():
+        arrived(0)
+
     loads[2].wait()
 
     y = jnp.zeros((2 * half * 16, 3 * LANES), F32)
@@ -632,10 +715,16 @@
 
     for stage in (1, 2):
         landed(plane_in.at[pl.ds(8 * stage, 2 * nx - 1)], plane_s.at[stage])
-        landed(line_in.at[pl.ds(stage * nz, nz - 1)], line_s.at[stage])
+        landed(line_in.at[pl.ds(stage * nz, len(line_steps(stage)))], line_s.at[stage])
+
+    landed(far_in, far_s)
     landed(params.at[pl.ds(0, nx - 1)], par_s)
     landed(r0.at[pl.ds(0, 5 * (2 * nx - 1))], x0_s)
-    landed(r0.at[pl.ds(0, 5 * 4 * nx)], z0_s)
+    for row, there in ((0, z < nz - 1), (1, z > 0)):
+        @pl.when(there)
+        def _():
+            landed(r0.at[pl.ds(0, 5 * 2 * nx)], z0_s.at[row])
+
     spread(a_sent, 0)
 
     @pl.when(boundary)
@@ -643,8 +732,18 @@
         spread(a_sent, 1)
 
     landed(x1.at[pl.ds(0, 3 * 3 * 6)], x1_s)
-    landed(x2.at[pl.ds(0, 2 * half * (2 * nx - 1))], x2_s)
-    landed(x2.at[pl.ds(0, 2 * 2 * nx)], e2_s)
+    landed(x2.at[pl.ds(0, 2 * half * (nx - 1))], x2_s.at[0])
+    landed(x2.at[pl.ds(0, 2 * nx)], e2_s.at[0])
+
+    @pl.when(has_next)
+    def _():
+        landed(x2.at[pl.ds(0, 2 * half)], x2_s.at[1])
+        landed(x2.at[pl.ds(0, 2 * nx)], e2_s.at[1])
+
+    @pl.when(has_past)
+    def _():
+        landed(x2.at[pl.ds(0, 2 * half * (nx - 1))], x2_s.at[2])
+
     last.wait()
 
     @pl.when(c == 0)
@@ -695,6 +794,7 @@
             pltpu.VMEM((3 * nz, 1, LANES), F32),
             pltpu.VMEM((nz * nx * 2, 1, LANES), F32),
             pltpu.VMEM((1, 1, LANES), F32),
+            pltpu.VMEM((3 * 2 * nx, 1, LANES), F32),
             dma((10,)),
             dma((3,)),
             dma,
@@ -706,17 +806,19 @@
             dma((3,)),
             dma((3,)),
             dma,
+            dma,
+            dma,
             dma((2 * nx,)),
-            dma,
+            dma((2,)),
             dma((4 * nx,)),
             dma((2 * half + 2,)),
             dma((10,)),
             dma,
             dma((nx,)),
-            dma,
+            dma((3,)),
             dma((2 * nx,)),
             dma((2,)),
-            dma,
+            dma((2,)),
             dma((2 * nx,)),
             dma,
             dma,

time: 64.3 us -> 63.4 us (0.986)
  Pallas kernels: 63.5 us -> 62.6 us
    pallas_call x1, Pallas kernels: 63.5 us -> 62.6 us  [body(): pl.pallas_call(functools.partial(kernel, nz, nx), out_shape=jax.ShapeDtyp...]
where the time goes in v6:
time: 63.4 us; the launch traced here: 63.3 us
  Pallas kernels  62.6 us (99%)
    pallas_call x1, Pallas kernels, body(): pl.pallas_call(functools.partial(kernel, nz, nx), out_shape=jax.ShapeDtyp...  62.6 us

profile of v6, /device:TPU:33, one launch (start us, length us, event | category | flops | bytes accessed | tf_op | source)
XLA Modules:
  0.0 63.3 jit_solution(12922401464998846788)
XLA Ops:
  0.0 62.6 %shard_map.127 = bf16[2,8,16,128]{3,2,1,0:T(8,128)(2,1)S(1)} custom-call(bf16[8,16,128]{2,1,0:T(8,128)(2,1)} %bitcast.18, f32[1,128]{1,0:T(1,128)} %bitcast.19, f32[1,128]{1,0:T(1,128)} %bitcast.20, bf16[27,512,128]{2,1,0:T(8,128)(2,1)} %bitcast.15, f32[1,128]{1,0:T(1,128)} %bitcast.21, f32[1,128]{1,0:T(1,128)} %bitcast.22, f32[1,128]{1,0:T(1,128)} %bitcast.23, ...), custom_call_target="tpu_custom_call" | custom-call | tf_op jit(solution)/shard_map/pallas_call | solution.py:768
  62.6 0.6 copy.15

commit v7 on v6

--- a/solution.py
+++ b/solution.py
@@ -123,6 +123,7 @@
     act1,
     act2,
     scales,
+    summed,
     middle,
     hidden,
     give,
@@ -283,15 +284,20 @@
             landed(hub_in.at[pl.ds(0, nz * nx * 2 - 1)], hub_r)
             total_row[0] = jnp.sum(hub_in[...], axis=0)
 
-            def far_first(k, carry):
-                step = (k + 1) // 2
-                dz = half + step * (2 * lax.rem(k, 2) - 1)
+            def send(dz):
                 remote(
                     total_row.at[0], total_row.at[0], line_s.at[0], line_r.at[0], peer(dz, 0, c)
                 ).start()
+
+            send(nz - 1)
+            send(1)
+
+            def far_first(k, carry):
+                step = (k + 1) // 2
+                send(half + step * (2 * lax.rem(k, 2) - 1))
                 return carry
 
-            lax.fori_loop(0, nz - 1, far_first, 0)
+            lax.fori_loop(0, nz - 3, far_first, 0)
 
     def hub_total():
         @pl.when(z != hub)
@@ -677,11 +683,25 @@
                     for fr in range(2):
                         act2[pair, 2 * own_frames + fr, lo:hi, :, k * LANES : (k + 1) * LANES] = part[:, fr]
         for di in range(3):
-            for dt in range(3):
+            for dt in (1, 2):
                 y = y + dot(
                     flat(act2[pair, dt : dt + 2, di : di + half]),
                     taps(w2, dt, di, (2 * pair, 2 * pair + 1)),
                 )
+    summed[...] = y
+
+    @pl.when(has_past)
+    def _():
+        y = summed[...]
+        for pair in range(nx // 2):
+            for di in range(3):
+                y = y + dot(
+                    flat(act2[pair, 0:2, di : di + half]),
+                    taps(w2, 0, di, (2 * pair, 2 * pair + 1)),
+                )
+        summed[...] = y
+
+    y = summed[...]
     mixed = column_sum(y.reshape(2 * half, 16, 3 * LANES)).reshape(2, half, 16, LANES)
     doubled = x1[pl.ds(x * 20 + 2, 2 * half)].astype(F32).reshape(half, 2, 16, LANES)[:, 1]
     final = doubled[None] + mixed + vectors[8].reshape(1, 1, 1, LANES)
@@ -784,6 +804,7 @@
             pltpu.VMEM((nx // 2, 2, half + 2, 16, 2 * LANES), BF),
             pltpu.VMEM((nx // 2, 4, half + 2, 16, 2 * LANES), BF),
             pltpu.VMEM((2 * nx, 1, LANES), F32),
+            pltpu.VMEM((2 * half * 16, 3 * LANES), F32),
             pltpu.VMEM((half, 16, LANES), BF),
             pltpu.VMEM((2 * half, 16, LANES), BF),
             pltpu.VMEM((2, half // 2, 16, LANES), BF),

time: 63.4 us -> 63.2 us (level)
  no operation moved by 1% of the time
where the time goes in v7:
time: 63.2 us; the launch traced here: 63 us
  Pallas kernels  62.4 us (99%)
    pallas_call x1, Pallas kernels, body(): pl.pallas_call(functools.partial(kernel, nz, nx), out_shape=jax.ShapeDtyp...  62.4 us

profile of v7, /device:TPU:33, one launch (start us, length us, event | category | flops | bytes accessed | tf_op | source)
XLA Modules:
  0.0 63.0 jit_solution(9098363795450782893)
XLA Ops:
  0.0 62.4 %shard_map.127 = bf16[2,8,16,128]{3,2,1,0:T(8,128)(2,1)S(1)} custom-call(bf16[8,16,128]{2,1,0:T(8,128)(2,1)} %bitcast.18, f32[1,128]{1,0:T(1,128)} %bitcast.19, f32[1,128]{1,0:T(1,128)} %bitcast.20, bf16[27,512,128]{2,1,0:T(8,128)(2,1)} %bitcast.15, f32[1,128]{1,0:T(1,128)} %bitcast.21, f32[1,128]{1,0:T(1,128)} %bitcast.22, f32[1,128]{1,0:T(1,128)} %bitcast.23, ...), custom_call_target="tpu_custom_call" | custom-call | tf_op jit(solution)/shard_map/pallas_call | solution.py:788
  62.4 0.6 %copy.15 = bf16[2,16,8,128]{3,2,1,0:T(8,128)(2,1)} copy(bf16[2,16,8,128]{3,2,1,0:T(8,128)(2,1)S(1)} %bitcast.14) | data formatting | bytes 131072

commit v8 on v7

--- a/solution.py
+++ b/solution.py
@@ -195,7 +195,7 @@
     for copy in inputs:
         copy.start()
 
-    hub = 1
+    hub = 2
     barrier = pltpu.get_barrier_semaphore()
 
     def greet(dz, dx, col):

time: 63.2 us -> 63 us (level)
  no operation moved by 1% of the time
where the time goes in v8:
time: 63 us; the launch traced here: 62.8 us
  Pallas kernels  62.2 us (99%)
  local copies, waits for them, and re-layouts  0.63 us (1%)
    pallas_call x1, Pallas kernels, body(): pl.pallas_call(functools.partial(kernel, nz, nx), out_shape=jax.ShapeDtyp...  62.2 us

profile of v8, /device:TPU:33, one launch (start us, length us, event | category | flops | bytes accessed | tf_op | source)
XLA Modules:
  0.0 62.8 jit_solution(15029570632438735235)
XLA Ops:
  0.0 62.2 %shard_map.127 = bf16[2,8,16,128]{3,2,1,0:T(8,128)(2,1)S(1)} custom-call(bf16[8,16,128]{2,1,0:T(8,128)(2,1)} %bitcast.18, f32[1,128]{1,0:T(1,128)} %bitcast.19, f32[1,128]{1,0:T(1,128)} %bitcast.20, bf16[27,512,128]{2,1,0:T(8,128)(2,1)} %bitcast.15, f32[1,128]{1,0:T(1,128)} %bitcast.21, f32[1,128]{1,0:T(1,128)} %bitcast.22, f32[1,128]{1,0:T(1,128)} %bitcast.23, ...), custom_call_target="tpu_custom_call" | custom-call | tf_op jit(solution)/shard_map/pallas_call | solution.py:788
  62.2 0.6 %copy.15 = bf16[2,16,8,128]{3,2,1,0:T(8,128)(2,1)} copy(bf16[2,16,8,128]{3,2,1,0:T(8,128)(2,1)S(1)} %bitcast.14) | data formatting | bytes 131072
